TPU v7x, 32 devices: a whole 2x2x4 slice. The times are simulated.
32 devices in a mesh: lat: 8 (over z, y), rad: 4 (over x, core).
Axes of the slice: x: 2, y: 2, z: 4, core: 2. Of those that a mesh axis runs over, the one named last changes fastest.
Arguments:
- displacement: float32 [64, 6144], P('rad', 'lat'), may hold values from -6 to 6
- surface_load: float32 [64, 6144], P('rad', 'lat'), may hold values from -6 to 6
- dens_grad: float32 [64, 6144], P('rad', 'lat'), may hold values from 0.5 to 2
- dens_ref: float32 [64], P('rad'), may hold values from 0.5 to 2
- relax_rate: float32 [64, 6144], P('rad', 'lat'), may hold values from 0.02 to 0.2
- basis: bfloat16 [2408, 6144], P(None, 'lat'), may hold values from -0.109375 to 0.109375
- neighbours: int32 [4, 6144], P(None, 'lat'), may hold values from 0 to 767
- green: float32 [49, 64, 64], replicated, may hold values from -2.5 to 2.5
Outputs:
- relaxed: float32 [64, 6144], P('rad', 'lat')
- step_sizes: float32 [3], replicated
Inputs may be any that keep to these rules, and one draw needn't show every extreme that they name: `neighbours`: indices of columns inside the same tile of 768 columns.
All inputs are finite; a program needn't handle non-finite values.
Results may differ from a plain program's by a relative error of at most 0.0045.
Values may be sent and summed in bfloat16 or wider, within the bound.
No kernel may reach another device: no remote copies, remote signals or barrier semaphores. Data moves between devices by JAX's collectives and lax.ppermute only.
A program may use at most 64 MiB of HBM per device.

v0:
```python
import jax
import jax.numpy as jnp
from jax import lax
from jax.sharding import PartitionSpec as P

DEG = 48
L = 64
ITERS = 3
KH = 2401


def extended(shard, sides, width):
    for axis, dim in sides:
        size, length = (lax.axis_size(axis), shard.shape[dim])
        up = [(i, (i + 1) % size) for i in range(size - 1)]
        down = [(j, i) for i, j in up]
        last = lax.slice_in_dim(shard, length - width, length, axis=dim)
        first = lax.slice_in_dim(shard, 0, width, axis=dim)
        before = lax.ppermute(last, axis, up)
        after = lax.ppermute(first, axis, down)
        shard = jnp.concatenate([before, shard, after], axis=dim)
    return shard


def apply_degrees(coefs, green_rows):
    blocks = []
    for degree in range(DEG + 1):
        rows = coefs[degree * degree : (degree + 1) * (degree + 1)]
        blocks.append(
            lax.dot_general(
                rows,
                green_rows[degree],
                (((1,), (1,)), ((), ())),
                precision=lax.Precision.HIGHEST,
                preferred_element_type=jnp.float32,
            )
        )
    blocks.append(jnp.zeros((coefs.shape[0] - KH, green_rows.shape[1]), jnp.float32))
    return jnp.concatenate(blocks, axis=0).astype(jnp.bfloat16)


def local(displacement, surface_load, dens_grad, dens_ref, relax_rate, basis, neighbours, green):
    u = displacement
    layers, columns = u.shape
    lat_count = lax.axis_size("lat")
    green_rows = lax.dynamic_slice_in_dim(green, lax.axis_index("rad") * layers, layers, 1)
    sizes = []
    for it in range(ITERS):
        padded = extended(u, (("rad", 0),), 1)
        rho = (dens_grad * u + dens_ref[:, None] * (padded[2:] - padded[:-2]) * 0.5).astype(
            jnp.bfloat16
        )
        partial_sums = lax.dot_general(
            basis, rho, (((1,), (1,)), ((), ())), preferred_element_type=jnp.float32
        )
        summed = lax.psum(partial_sums, "lat")
        coefs = lax.all_gather(summed, "rad", axis=1, tiled=True)
        phi = apply_degrees(coefs, green_rows)
        potential = lax.dot_general(
            phi, basis, (((0,), (0,)), ((), ())), preferred_element_type=jnp.float32
        )
        outer = extended(potential, (("rad", 0),), 1)
        force = (outer[2:] - outer[:-2]) * 0.5
        lap = jnp.sum(u[:, neighbours], axis=1) - 4.0 * u
        new = u + relax_rate * (surface_load + force + lap - u)
        squared = jnp.sum((new - u) ** 2)
        sizes.append(squared)
        u = new
    totals = jnp.stack(sizes)
    totals = lax.psum(totals, ("lat", "rad"))
    return (u, jnp.sqrt(totals / (L * columns * lat_count)))


def solution(mesh):
    placed = (
        P("rad", "lat"),
        P("rad", "lat"),
        P("rad", "lat"),
        P("rad"),
        P("rad", "lat"),
        P(None, "lat"),
        P(None, "lat"),
        P(),
    )
    return jax.shard_map(
        local, mesh=mesh, in_specs=placed, out_specs=(P("rad", "lat"), P()), check_vma=False
    )
```

profile of v0, /device:TPU:0, one launch (start us, length us, event | category | flops | bytes accessed | tf_op | source)
XLA Modules:
  0.0 424.7 jit_solution(13441633414190941219)
XLA Ops:
  7.2 0.9 fusion.406
  8.1 2.4 collective-permute-start.1
  10.5 1.3 collective-permute-start
  11.8 3.8 collective-permute-done
  15.6 3.9 convolution_bitcast_fusion.2
  19.7 72.3 %all-reduce.4.cloned.1.call-done = f32[2408,16]{0,1:T(8,128)} async-done(((f32[2408,16]{0,1:T(8,128)}), f32[2408,16]{0,1:T(8,128)}) %all-reduce.4.cloned.1.call-update) | async-done | bytes 154128 | tf_op jit(solution)/shard_map/psum | solution.py:56
  92.0 7.9 %all_gather.9 = f32[2408,64]{0,1:T(8,128)S(1)} all-gather(f32[2408,16]{0,1:T(8,128)} %all-reduce.4.cloned.1.call-done), channel_id=1, replica_groups=mesh['lat'=8,'rad'=4] {'rad'}, dimensions={1}, use_global_device_ids=true | all-gather | bytes 770560 | tf_op jit(solution)/shard_map/all_gather | solution.py:57
  100.2 0.3 convolution_convert_fusion.143
  100.6 0.3 convolution_convert_fusion.140
  101.0 0.3 convolution_convert_fusion.139
  101.4 0.3 convolution_convert_fusion.134
  101.8 0.3 convolution_convert_fusion.133
  102.2 0.3 convolution_convert_fusion.132
  102.6 0.3 convolution_convert_fusion.131
  103.0 0.2 convolution_convert_fusion.130
  103.4 0.2 convolution_convert_fusion.128
  104.1 0.2 convolution_convert_fusion.125
  112.0 2.7 fusion.407
  114.7 2.3 collective-permute-start.3
  116.9 1.3 collective-permute-start.2
  118.4 10.8 %gather_fusion = f32[3072,16]{1,0:T(8,128)} fusion(f32[16,768]{0,1:T(8,128)S(1)} %copy.24, s32[3072]{0:T(1024)S(1)} %broadcast_clamp_fusion), kind=kCustom, calls=%fused_computation | custom fusion | bytes 405504 | tf_op jit(solution)/shard_map/gather | solution.py:64
  129.3 1.6 reduce.3
  131.1 3.0 collective-permute-start.5
  134.1 1.3 collective-permute-start.4
  135.5 2.8 collective-permute-done.4
  138.3 3.8 convolution_bitcast_fusion.1
  142.1 70.9 %all-reduce.6.cloned.1.call-done = f32[2408,16]{0,1:T(8,128)} async-done(((f32[2408,16]{0,1:T(8,128)}), f32[2408,16]{0,1:T(8,128)}) %all-reduce.6.cloned.1.call-update) | async-done | bytes 154128 | tf_op jit(solution)/shard_map/psum | solution.py:56
  213.1 7.9 %all_gather.10 = f32[2408,64]{0,1:T(8,128)S(1)} all-gather(f32[2408,16]{0,1:T(8,128)} %all-reduce.6.cloned.1.call-done), channel_id=1, replica_groups=mesh['lat'=8,'rad'=4] {'rad'}, dimensions={1}, use_global_device_ids=true | all-gather | bytes 770560 | tf_op jit(solution)/shard_map/all_gather | solution.py:57
  221.1 0.3 convolution_convert_fusion.142
  221.3 0.3 convolution_convert_fusion.138
  221.6 0.3 convolution_convert_fusion.137
  221.9 0.3 convolution_convert_fusion.89
  222.2 0.3 convolution_convert_fusion.88
  222.5 0.3 convolution_convert_fusion.87
  222.8 0.3 convolution_convert_fusion.86
  223.1 0.2 convolution_convert_fusion.85
  233.1 2.6 fusion.408
  235.7 2.3 collective-permute-start.7
  238.0 1.3 collective-permute-start.6
  239.4 10.8 %gather_fusion.1 = f32[3072,16]{1,0:T(8,128)} fusion(f32[16,768]{0,1:T(8,128)S(1)} %copy.34, s32[3072]{0:T(1024)S(1)} %broadcast_clamp_fusion), kind=kCustom, calls=%fused_computation.1 | custom fusion | bytes 405504 | tf_op jit(solution)/shard_map/gather | solution.py:64
  250.3 1.6 reduce.4
  252.0 3.0 collective-permute-start.9
  255.1 1.3 collective-permute-start.8
  256.4 2.8 collective-permute-done.8
  259.2 3.8 convolution_bitcast_fusion
  263.0 71.0 %all-reduce.8.cloned.1.call-done = f32[2408,16]{0,1:T(8,128)} async-done(((f32[2408,16]{0,1:T(8,128)}), f32[2408,16]{0,1:T(8,128)}) %all-reduce.8.cloned.1.call-update) | async-done | bytes 154128 | tf_op jit(solution)/shard_map/psum | solution.py:56
  334.0 8.1 %all_gather.11 = f32[2408,64]{0,1:T(8,128)S(1)} all-gather(f32[2408,16]{0,1:T(8,128)} %all-reduce.8.cloned.1.call-done), channel_id=1, replica_groups=mesh['lat'=8,'rad'=4] {'rad'}, dimensions={1}, use_global_device_ids=true | all-gather | bytes 770560 | tf_op jit(solution)/shard_map/all_gather | solution.py:57
  342.2 0.3 convolution_convert_fusion.141
  342.4 0.3 convolution_convert_fusion.136
  342.7 0.3 convolution_convert_fusion.135
  343.0 0.3 convolution_convert_fusion.44
  343.3 0.3 convolution_convert_fusion.43
  343.6 0.3 convolution_convert_fusion.42
  343.9 0.3 convolution_convert_fusion.41
  344.2 0.2 convolution_convert_fusion.40
  354.2 2.6 fusion.409
  356.8 2.3 collective-permute-start.11
  359.1 1.3 collective-permute-start.10
  360.6 10.8 %gather_fusion.2 = f32[3072,16]{1,0:T(8,128)} fusion(f32[16,768]{0,1:T(8,128)S(1)} %copy.44, s32[3072]{0:T(1024)S(1)} %broadcast_clamp_fusion), kind=kCustom, calls=%fused_computation.2 | custom fusion | bytes 405504 | tf_op jit(solution)/shard_map/gather | solution.py:64
  371.4 1.6 reduce.5
  373.1 1.4 multiply_reduce_fusion.2
  374.4 2.0 pad_maximum_fusion.12
  376.4 41.3 %psum.31 = f32[3]{0:T(128)S(1)} all-reduce(f32[3]{0:T(128)S(1)} %pad_maximum_fusion.12), channel_id=1, replica_groups=mesh['lat'=8,'rad'=4] {'lat','rad'}, use_global_device_ids=true, to_apply=%region_9.0 | all-reduce | flops 3 | bytes 24 | tf_op jit(solution)/shard_map/psum | solution.py:70
  417.7 0.5 multiply_sqrt_fusion
  (197 shorter events, 30.2 us)
Async XLA Ops:
  7.2 92.8 %copy-start = (f32[49,64,64]{2,1,0:T(8,128)S(1)}, f32[49,64,64]{2,1,0:T(8,128)}, u32[]{:S(2)}) copy-start(f32[49,64,64]{2,1,0:T(8,128)} %param.15) | copy-start | bytes 2408452
  7.2 84.8 %all-reduce.4.cloned.1.call-start = ((), (), s32[]{:S(2)}) async-start(), calls=%async_computation | async-start | bytes 311296 | tf_op jit(solution)/shard_map/psum | solution.py:56
  8.1 3.7 collective-permute-start.1
  10.5 5.2 %collective-permute-start = (f32[1,768]{1,0:T(1,128)S(1)}, f32[1,768]{1,0:T(1,128)S(1)}, u32[]{:S(2)}, u32[]{:S(2)}) collective-permute-start(f32[1,768]{1,0:T(1,128)S(1)} %get-tuple-element.16), channel_id=1, source_target_pairs={{1,0},{2,1},{3,2},{5,4},{6,5},{7,6},{9,8},{10,9},{11,10},{13,12},{... | collective-permute-start | bytes 9224 | tf_op jit(solution)/shard_map/ppermute | solution.py:20
  11.8 7.8 %copy-start.5 = (s32[4,768]{1,0:T(4,128)S(1)}, s32[4,768]{1,0:T(4,128)}, u32[]{:S(2)}) copy-start(s32[4,768]{1,0:T(4,128)} %param.14) | copy-start | bytes 36868
  19.6 193.5 %all-reduce.6.cloned.1.call-start = ((), (), s32[]{:S(2)}) async-start(), calls=%async_computation.1 | async-start | bytes 311296 | tf_op jit(solution)/shard_map/psum | solution.py:56
  112.0 6.3 %copy-start.1 = (f32[16,768]{1,0:T(8,128)S(1)}, f32[16,768]{1,0:T(8,128)}, u32[]{:S(2)}) copy-start(f32[16,768]{1,0:T(8,128)} %param.8) | copy-start | bytes 147460
  114.7 16.3 %collective-permute-start.3 = (f32[1,768]{1,0:T(1,128)S(1)}, f32[1,768]{1,0:T(1,128)S(1)}, u32[]{:S(2)}, u32[]{:S(2)}) collective-permute-start(f32[1,768]{1,0:T(1,128)S(1)} %get-tuple-element.15), channel_id=1, source_target_pairs={{0,1},{1,2},{2,3},{4,5},{5,6},{6,7},{8,9},{9,10},{10,11},{12,13},{... | collective-permute-start | bytes 9224 | tf_op jit(solution)/shard_map/ppermute | solution.py:19
  116.9 14.1 %collective-permute-start.2 = (f32[1,768]{1,0:T(1,128)S(1)}, f32[1,768]{1,0:T(1,128)S(1)}, u32[]{:S(2)}, u32[]{:S(2)}) collective-permute-start(f32[1,768]{1,0:T(1,128)S(1)} %get-tuple-element.14), channel_id=1, source_target_pairs={{1,0},{2,1},{3,2},{5,4},{6,5},{7,6},{9,8},{10,9},{11,10},{13,12},{... | collective-permute-start | bytes 9224 | tf_op jit(solution)/shard_map/ppermute | solution.py:20
  129.3 1.8 copy-start.3
  129.3 1.8 copy-start.4
  129.3 9.0 %copy-start.2 = (f32[16,768]{1,0:T(8,128)S(1)}, f32[16,768]{1,0:T(8,128)}, u32[]{:S(2)}) copy-start(f32[16,768]{1,0:T(8,128)} %param.10) | copy-start | bytes 147460
  129.3 9.0 %copy-start.6 = (f32[16]{0:T(128)S(1)}, f32[16]{0:T(128)}, u32[]{:S(2)}) copy-start(f32[16]{0:T(128)} %param.11) | copy-start | bytes 196
  131.1 4.3 %collective-permute-start.5 = (f32[1,768]{1,0:T(1,128)S(1)}, f32[1,768]{1,0:T(1,128)S(1)}, u32[]{:S(2)}, u32[]{:S(2)}) collective-permute-start(f32[1,768]{1,0:T(1,128)S(1)} %get-tuple-element.13), channel_id=1, source_target_pairs={{0,1},{1,2},{2,3},{4,5},{5,6},{6,7},{8,9},{9,10},{10,11},{12,13},{... | collective-permute-start | bytes 9224 | tf_op jit(solution)/shard_map/ppermute | solution.py:19
  134.1 4.1 collective-permute-start.4
  142.1 191.9 %all-reduce.8.cloned.1.call-start = ((), (), s32[]{:S(2)}) async-start(), calls=%async_computation.2 | async-start | bytes 311296 | tf_op jit(solution)/shard_map/psum | solution.py:56
  235.7 16.2 %collective-permute-start.7 = (f32[1,768]{1,0:T(1,128)S(1)}, f32[1,768]{1,0:T(1,128)S(1)}, u32[]{:S(2)}, u32[]{:S(2)}) collective-permute-start(f32[1,768]{1,0:T(1,128)S(1)} %get-tuple-element.11), channel_id=1, source_target_pairs={{0,1},{1,2},{2,3},{4,5},{5,6},{6,7},{8,9},{9,10},{10,11},{12,13},{... | collective-permute-start | bytes 9224 | tf_op jit(solution)/shard_map/ppermute | solution.py:19
  238.0 14.0 %collective-permute-start.6 = (f32[1,768]{1,0:T(1,128)S(1)}, f32[1,768]{1,0:T(1,128)S(1)}, u32[]{:S(2)}, u32[]{:S(2)}) collective-permute-start(f32[1,768]{1,0:T(1,128)S(1)} %get-tuple-element.10), channel_id=1, source_target_pairs={{1,0},{2,1},{3,2},{5,4},{6,5},{7,6},{9,8},{10,9},{11,10},{13,12},{... | collective-permute-start | bytes 9224 | tf_op jit(solution)/shard_map/ppermute | solution.py:20
  252.0 4.3 %collective-permute-start.9 = (f32[1,768]{1,0:T(1,128)S(1)}, f32[1,768]{1,0:T(1,128)S(1)}, u32[]{:S(2)}, u32[]{:S(2)}) collective-permute-start(f32[1,768]{1,0:T(1,128)S(1)} %get-tuple-element.9), channel_id=1, source_target_pairs={{0,1},{1,2},{2,3},{4,5},{5,6},{6,7},{8,9},{9,10},{10,11},{12,13},{... | collective-permute-start | bytes 9224 | tf_op jit(solution)/shard_map/ppermute | solution.py:19
  255.1 4.1 collective-permute-start.8
  356.8 16.2 %collective-permute-start.11 = (f32[1,768]{1,0:T(1,128)S(1)}, f32[1,768]{1,0:T(1,128)S(1)}, u32[]{:S(2)}, u32[]{:S(2)}) collective-permute-start(f32[1,768]{1,0:T(1,128)S(1)} %get-tuple-element.7), channel_id=1, source_target_pairs={{0,1},{1,2},{2,3},{4,5},{5,6},{6,7},{8,9},{9,10},{10,11},{12,13},{... | collective-permute-start | bytes 9224 | tf_op jit(solution)/shard_map/ppermute | solution.py:19
  359.1 14.0 %collective-permute-start.10 = (f32[1,768]{1,0:T(1,128)S(1)}, f32[1,768]{1,0:T(1,128)S(1)}, u32[]{:S(2)}, u32[]{:S(2)}) collective-permute-start(f32[1,768]{1,0:T(1,128)S(1)} %get-tuple-element.6), channel_id=1, source_target_pairs={{1,0},{2,1},{3,2},{5,4},{6,5},{7,6},{9,8},{10,9},{11,10},{13,12},{... | collective-permute-start | bytes 9224 | tf_op jit(solution)/shard_map/ppermute | solution.py:20
Sparse Core Ops, SparseCore 0:
  19.7 72.2 all-reduce.3
  142.2 70.8 all-reduce.5
  263.1 70.8 all-reduce.7
where the time goes:
time: 426 us; the launch traced here: 425 us
  waiting for transfers between devices  224 us (53%)
  blocking collectives  65.1 us (15%)
  matrix products  52.3 us (12%)
  local copies, waits for them, and re-layouts  37.5 us (9%)
  starting transfers between devices  23.1 us (5%)
  between operations  14.2 us (3%)
  other arithmetic  8.64 us (2%)
    psum x3, waiting for transfers between devices, local(): summed = lax.psum(partial_sums, 'lat')  214 us
    psum x1, blocking collectives, local(): totals = lax.psum(totals, ('lat', 'rad'))  41.3 us
    dot_general x147, matrix products, apply_degrees(): lax.dot_general(rows, green_rows[degree], (((1,), (1,)), ((), ())), preci...  32.9 us
    gather x3, local copies, waits for them, and re-layouts, local(): lap = jnp.sum(u[:, neighbours], axis=1) - 4.0 * u  32.5 us
    all_gather x3, blocking collectives, local(): coefs = lax.all_gather(summed, 'rad', axis=1, tiled=True)  23.9 us
    ppermute x6, starting transfers between devices, extended(): before = lax.ppermute(last, axis, up)  15.2 us
    dot_general x3, matrix products, local(): lax.dot_general(basis, rho, (((1,), (1,)), ((), ())), preferred_element_t...  11.5 us
    ppermute x6, waiting for transfers between devices, extended(): after = lax.ppermute(first, axis, down)  9.47 us
  transfers between devices with their start and end apart: 15, of which 6 were waited for; matrix products, arithmetic and copies ran while one was open for 9% of the time, Pallas kernels for 0%

commit v1 on v0

v1 whole, which is shorter than its diff:
```python
import jax
import jax.numpy as jnp
from jax import lax
from jax.experimental import pallas as pl
from jax.experimental.pallas import tpu as pltpu
from jax.sharding import PartitionSpec as P

DEG = 48
L = 64
ITERS = 3
KH = 2401
LANES = 128
HALO = 8

F32, BF16 = jnp.float32, jnp.bfloat16
NT = (((1,), (1,)), ((), ()))
NN = (((1,), (0,)), ((), ()))


def degree_of(k):
    d = 0
    while (d + 1) * (d + 1) <= k:
        d += 1
    return d


def chunks_of(slots, chunk):
    return [(k, min(k + chunk, slots)) for k in range(0, slots, chunk)]


def bf16_parts(x, count):
    parts = []
    for _ in range(count):
        part = x.astype(BF16)
        parts.append(part)
        x = x - part.astype(F32)
    return parts


def build_counts(nb_ref, counts_ref):
    tile = counts_ref.shape[1]
    rows = 32

    def body(b, carry):
        at = pl.multiple_of(b * rows, rows)
        source = lax.broadcasted_iota(jnp.int32, (rows, tile), 0) + at
        total = jnp.zeros((rows, tile), F32)
        for j in range(nb_ref.shape[0]):
            total = total + (source == nb_ref[j : j + 1, :]).astype(F32)
        counts_ref[pl.ds(at, rows), :] = total.astype(BF16)
        return carry

    lax.fori_loop(0, tile // rows, body, 0)


def analyse(u, own, grad_ref, dens_ref, basis_ref, send_ref, squares, chunk):
    rows = u.shape[0]
    above = pltpu.roll(u, rows - 1, 0)
    below = pltpu.roll(u, 1, 0)
    step = (above[:own] - below[:own]) * 0.5
    rho = (grad_ref[...] * u[:own] + dens_ref[...] * step).astype(BF16)
    pieces = chunks_of(basis_ref.shape[0], chunk)
    lane = lax.broadcasted_iota(jnp.int32, (own, LANES), 1)
    row = lax.broadcasted_iota(jnp.int32, (own, LANES), 0)
    if squares is None:
        tail = jnp.zeros((own, LANES), BF16)
    else:
        high, low = [p.astype(F32) for p in bf16_parts(squares, 2)]
        tail = jnp.where(lane == chunk, high, jnp.where(lane == chunk + 1, low, 0.0))
        tail = jnp.where(row == 0, tail, 0.0).astype(BF16)
    for d in range(send_ref.shape[0]):
        send_ref[d] = tail
    for d, (start, end) in enumerate(pieces):
        part = lax.dot_general(rho, basis_ref[start:end, :], NT, preferred_element_type=F32)
        send_ref[d, :, 0 : end - start] = part.astype(BF16)


def advance(recv_ref, u_ref, load_ref, rate_ref, basis_ref, counts_ref, own, chunk):
    u = u_ref[...]
    rows = u.shape[0]
    force = jnp.zeros(u.shape, F32)
    for d, (start, end) in enumerate(chunks_of(basis_ref.shape[0], chunk)):
        force = force + lax.dot_general(
            recv_ref[d][:, 0 : end - start], basis_ref[start:end, :], NN, preferred_element_type=F32
        )
    parts = jnp.concatenate([p.astype(F32) for p in bf16_parts(u, 3)], axis=0).astype(BF16)
    sums = lax.dot_general(parts, counts_ref[...], NN, preferred_element_type=F32)
    lap = sums[:rows] + sums[rows : 2 * rows] + sums[2 * rows :] - 4.0 * u
    new = u + rate_ref[...] * (load_ref[...] + force + lap - u)
    change = (new - u)[:own]
    squares = jnp.sum(jnp.sum(change * change, axis=0, keepdims=True), axis=1, keepdims=True)
    return new, squares


def first_kernel(own, chunk, u0, load0, rate0, halo, grad, dens, basis, nb, u, load, rate, counts, send):
    for i, (block, out) in enumerate(((u0, u), (load0, load), (rate0, rate))):
        row = lax.broadcasted_iota(jnp.int32, (HALO, block.shape[1]), 0)
        edge = jnp.where(row == 0, halo[0, i : i + 1, :], 0.0)
        edge = jnp.where(row == HALO - 1, halo[1, i : i + 1, :], edge)
        out[...] = jnp.concatenate([block[...], edge], axis=0)
    build_counts(nb, counts)
    analyse(u[...], own, grad, dens, basis, send, None, chunk)


def middle_kernel(own, chunk, recv, u, load, rate, grad, dens, basis, counts, u_out, send):
    new, squares = advance(recv, u, load, rate, basis, counts, own, chunk)
    u_out[...] = new
    analyse(new, own, grad, dens, basis, send, squares, chunk)


def last_kernel(own, chunk, recv, u, load, rate, basis, counts, relaxed, send):
    new, squares = advance(recv, u, load, rate, basis, counts, own, chunk)
    relaxed[...] = new[:own]
    send[...] = jnp.broadcast_to(squares.reshape(1, 1, 1), send.shape)


def harmonic_kernel(lats, rads, chunk, degrees, first, recv, green, send, total, phi_ref):
    own = recv.shape[1]
    layers = rads * own
    device = lax.axis_index("lat") * rads + lax.axis_index("rad")
    blocks = []
    for j in range(rads):
        block = recv[j].astype(F32)
        for i in range(1, lats):
            block = block + recv[i * rads + j].astype(F32)
        blocks.append(block)
    coefs = jnp.concatenate(blocks, axis=0)
    lane = lax.broadcasted_iota(jnp.int32, (layers, LANES), 1)
    extra = jnp.where(lane >= chunk, coefs, 0.0)
    squares = jnp.sum(jnp.sum(extra, axis=0, keepdims=True), axis=1, keepdims=True)
    total[...] = jnp.broadcast_to(squares, total.shape)
    every = lax.dot_general(
        green[...], coefs, NN, precision=lax.Precision.HIGHEST, preferred_element_type=F32
    )
    k = lane + device * chunk
    low = first(device)
    phi = jnp.zeros((layers, LANES), F32)
    for n in range(degrees):
        degree = low + n
        mine = (k >= degree * degree) & (k < (degree + 1) * (degree + 1)) & (lane < chunk)
        phi = phi + jnp.where(mine, every[n * layers : (n + 1) * layers], 0.0)
    side = own + HALO
    edge = jnp.zeros((side, LANES), F32)
    phi_ref[0:side, :] = edge
    phi_ref[side : side + layers, :] = phi
    phi_ref[side + layers : side + layers + side, :] = edge
    row = lax.broadcasted_iota(jnp.int32, (side, LANES), 0)
    for j in range(rads):
        at = side + j * own
        here = phi_ref[at + 1 : at + 1 + side, :] - phi_ref[at - 1 : at - 1 + side, :]
        before = phi_ref[at : at + 1, :] - phi_ref[at - 2 : at - 1, :]
        slab = (jnp.where(row == side - 1, before, here) * 0.5).astype(BF16)
        for i in range(lats):
            send[i * rads + j] = slab


def local(displacement, surface_load, dens_grad, dens_ref, relax_rate, basis, neighbours, green):
    own, columns = displacement.shape
    slots = basis.shape[0]
    lats, rads = lax.axis_size("lat"), lax.axis_size("rad")
    devices = lats * rads
    both = ("lat", "rad")
    chunk = -(-slots // devices)
    chunk = -(-chunk // 16) * 16
    rows = own + HALO
    layers = rads * own
    firsts = [min(degree_of(k), DEG) for k in range(0, devices * chunk, chunk)]
    lasts = [min(degree_of(k + chunk - 1), DEG) for k in range(0, devices * chunk, chunk)]
    degrees = max(b - a + 1 for a, b in zip(firsts, lasts))

    def first(device):
        k = device * chunk
        count = jnp.int32(0)
        for d in range(1, DEG + 1):
            count = count + (k >= d * d).astype(jnp.int32)
        return jnp.minimum(count, DEG + 1 - degrees)

    device = lax.axis_index("lat") * rads + lax.axis_index("rad")
    mine = lax.dynamic_slice_in_dim(green, first(device), degrees, 0).reshape(degrees * L, L)

    up = [(i, i + 1) for i in range(rads - 1)]
    down = [(i + 1, i) for i in range(rads - 1)]
    stack = (displacement, surface_load, relax_rate)
    tops = jnp.concatenate([a[own - 1 :] for a in stack], axis=0)
    bottoms = jnp.concatenate([a[:1] for a in stack], axis=0)
    before = lax.ppermute(tops, "rad", up)
    after = lax.ppermute(bottoms, "rad", down)
    halo = jnp.stack([after, before])
    dens = dens_ref[:, None]

    def struct(shape, dtype=F32):
        return jax.ShapeDtypeStruct(shape, dtype)

    field = struct((rows, columns))
    partial = struct((devices, own, LANES), BF16)
    back = struct((devices, rows, LANES), BF16)

    def bound(kernel, *args):
        def body(*refs):
            kernel(*args, *refs)

        return body

    def exchange(x):
        return lax.all_to_all(x, both, 0, 0, tiled=True)

    u, load, rate, counts, send = pl.pallas_call(
        bound(first_kernel, own, chunk),
        out_shape=(field, field, field, struct((columns, columns), BF16), partial),
        name="first",
    )(displacement, surface_load, relax_rate, halo, dens_grad, dens, basis, neighbours)
    totals = []
    for it in range(ITERS):
        recv = exchange(send)
        send, total = pl.pallas_call(
            bound(harmonic_kernel, lats, rads, chunk, degrees, first),
            out_shape=(back, struct((8, LANES))),
            scratch_shapes=[pltpu.VMEM((layers + 2 * rows, LANES), F32)],
            name="harmonic",
        )(recv, mine)
        totals.append(total[0, 0])
        recv = exchange(send)
        if it < ITERS - 1:
            u, send = pl.pallas_call(
                bound(middle_kernel, own, chunk), out_shape=(field, partial), name="middle"
            )(recv, u, load, rate, dens_grad, dens, basis, counts)
        else:
            relaxed, send = pl.pallas_call(
                bound(last_kernel, own, chunk),
                out_shape=(struct((own, columns)), struct((devices, 1, LANES))),
                name="last",
            )(recv, u, load, rate, basis, counts)
    final = jnp.sum(exchange(send)[:, 0, 0])
    sums = jnp.stack(totals[1:] + [final])
    return (relaxed, jnp.sqrt(sums / (layers * columns * lats)))


def solution(mesh):
    placed = (
        P("rad", "lat"),
        P("rad", "lat"),
        P("rad", "lat"),
        P("rad"),
        P("rad", "lat"),
        P(None, "lat"),
        P(None, "lat"),
        P(),
    )
    return jax.shard_map(
        local, mesh=mesh, in_specs=placed, out_specs=(P("rad", "lat"), P()), check_vma=False
    )
```

time: 426 us -> 125 us (0.29)
  waiting for transfers between devices: 224 us -> 14.6 us
  matrix products: 52.3 us -> 0 us
  local copies, waits for them, and re-layouts: 37.5 us -> 6.75 us
  Pallas kernels: 0 us -> 26 us
  between operations: 14.2 us -> 0.93 us
  starting transfers between devices: 23.1 us -> 13.2 us
  blocking collectives: 65.1 us -> 59.5 us
  other arithmetic: 8.64 us -> 3.75 us
    psum x3 -> x0, waiting for transfers between devices: 214 us -> none  [local(): summed = lax.psum(partial_sums, 'lat')]
    all_to_all x0 -> x5, blocking collectives: none -> 59.5 us  [exchange(): return lax.all_to_all(x, both, 0, 0, tiled=True)]
    dot_general x153 -> x0, matrix products: 52.3 us -> none  [the longest x147 32.9 us: apply_degrees(): lax.dot_general(rows, green_rows[degree], (((1,), (1,)), ((), ())), preci...]
    psum x1 -> x0, blocking collectives: 41.3 us -> none  [local(): totals = lax.psum(totals, ('lat', 'rad'))]
    gather x3 -> x0, local copies, waits for them, and re-layouts: 32.5 us -> none  [local(): lap = jnp.sum(u[:, neighbours], axis=1) - 4.0 * u]
    pallas_call x0 -> x7, Pallas kernels: none -> 26 us  [the longest x2 10.4 us: local(): pl.pallas_call(bound(middle_kernel, own, chunk), out_shape=(field, partia...]
    all_gather x3 -> x0, blocking collectives: 23.9 us -> none  [local(): coefs = lax.all_gather(summed, 'rad', axis=1, tiled=True)]
    ppermute x12 -> x2, starting transfers between devices: 23 us -> 3.69 us  [the longest x1 2.4 us: local(): before = lax.ppermute(tops, 'rad', up)]
  transfers between devices with their start and end apart: 15 -> 4, of which waited for: 6 -> 3; matrix products, arithmetic and copies ran while one was open for 9% -> 4% of each run, Pallas kernels for 0% -> 0%
where the time goes in v1:
time: 125 us
  blocking collectives  59.5 us (48%)
  Pallas kernels  26 us (21%)
  waiting for transfers between devices  14.6 us (12%)
  starting transfers between devices  13.2 us (11%)
  local copies, waits for them, and re-layouts  6.75 us (5%)
  other arithmetic  3.75 us (3%)
    all_to_all x5, blocking collectives, exchange(): return lax.all_to_all(x, both, 0, 0, tiled=True)  59.5 us
    all_to_all x2, waiting for transfers between devices, exchange(): return lax.all_to_all(x, both, 0, 0, tiled=True)  12.1 us
    pallas_call x2, Pallas kernels, local(): pl.pallas_call(bound(middle_kernel, own, chunk), out_shape=(field, partia...  10.4 us
    all_to_all x2, starting transfers between devices, exchange(): return lax.all_to_all(x, both, 0, 0, tiled=True)  9.52 us
    pallas_call x3, Pallas kernels, local(): pl.pallas_call(bound(harmonic_kernel, lats, rads, chunk, degrees, first),...  6.38 us
    pallas_call x1, Pallas kernels, local(): pl.pallas_call(bound(first_kernel, own, chunk), out_shape=(field, field,...  5.01 us
    pallas_call x1, Pallas kernels, local(): pl.pallas_call(bound(last_kernel, own, chunk), out_shape=(struct((own, co...  4.15 us
    ppermute x1, waiting for transfers between devices, local(): after = lax.ppermute(bottoms, 'rad', down)  2.54 us
  transfers between devices with their start and end apart: 4, of which 3 were waited for; matrix products, arithmetic and copies ran while one was open for 4% of the time, Pallas kernels for 0%

profile of v1, /device:TPU:0, one launch (start us, length us, event | category | flops | bytes accessed | tf_op | source)
XLA Modules:
  0.0 124.8 jit_solution(8106435172954032208)
XLA Ops:
  0.6 0.0 copy-start
  0.6 0.9 fusion.3
  1.5 0.8 fusion.1
  2.4 2.4 %collective-permute-start.1 = (f32[3,768]{1,0:T(4,128)S(1)}, f32[3,768]{1,0:T(4,128)S(1)}, u32[]{:S(2)}, u32[]{:S(2)}) collective-permute-start(f32[3,768]{1,0:T(4,128)S(1)} %pad_maximum_fusion.2), channel_id=1, source_target_pairs={{0,1},{1,2},{2,3},{4,5},{5,6},{6,7},{8,9},{9,10},{10,11},{12,13},{... | collective-permute-start | bytes 27656 | tf_op jit(solution)/shard_map/ppermute | solution.py:186
  4.8 1.3 %collective-permute-start = (f32[3,768]{1,0:T(4,128)S(1)}, f32[3,768]{1,0:T(4,128)S(1)}, u32[]{:S(2)}, u32[]{:S(2)}) collective-permute-start(f32[3,768]{1,0:T(4,128)S(1)} %pad_maximum_fusion.1), channel_id=1, source_target_pairs={{1,0},{2,1},{3,2},{5,4},{6,5},{7,6},{9,8},{10,9},{11,10},{13,12},{... | collective-permute-start | bytes 27656 | tf_op jit(solution)/shard_map/ppermute | solution.py:187
  6.1 1.3 %copy.10.refs_5_ = f32[16,1]{1,0:T(8,128)} copy(f32[16,1]{0,1:T(1,128)} %bitcast.12) | data formatting | bytes 128 | tf_op jit(solution)/shard_map/broadcast_in_dim | solution.py:189
  7.4 0.0 collective-permute-done.1
  7.4 2.5 %collective-permute-done = f32[3,768]{1,0:T(4,128)S(1)} collective-permute-done((f32[3,768]{1,0:T(4,128)S(1)}, f32[3,768]{1,0:T(4,128)S(1)}, u32[]{:S(2)}, u32[]{:S(2)}) %collective-permute-start) | collective-permute-done | bytes 9248 | tf_op jit(solution)/shard_map/ppermute | solution.py:187
  9.9 0.6 pad_maximum_fusion.refs_3_
  10.6 5.0 %first.1 = (f32[24,768]{1,0:T(8,128)}, f32[24,768]{1,0:T(8,128)}, f32[24,768]{1,0:T(8,128)}, bf16[768,768]{1,0:T(8,128)(2,1)}, bf16[32,16,128]{2,1,0:T(8,128)(2,1)}) custom-call(f32[16,768]{1,0:T(8,128)} %refs_0_.1, f32[16,768]{1,0:T(8,128)} %refs_1_.1, f32[16,768]{1,0:T(8,128)} %refs_2_.1, f32[2,3,768]{2,1,0:T(4,128)} %pad_maximum_fusion.refs_3_, ...), custom_call_target="tpu_custom_call" | custom-call | tf_op jit(solution)/shard_map/first/pallas_call | solution.py:207
  15.6 7.0 %all-to-all-start = ((bf16[32,16,128]{2,1,0:T(8,128)(2,1)}), bf16[32,16,128]{2,1,0:T(8,128)(2,1)S(1)}, u32[]{:S(2)}, u32[]{:S(2)}) async-start(bf16[32,16,128]{2,1,0:T(8,128)(2,1)} %get-tuple-element.18), calls=%async_computation | async-start | bytes 262144 | tf_op jit(solution)/shard_map/all_to_all | solution.py:205
  22.8 0.0 copy-done
  22.8 0.7 constant_dynamic-slice_fusion
  23.5 7.2 %all-to-all-done.refs_0_ = bf16[32,16,128]{2,1,0:T(8,128)(2,1)S(1)} async-done(((bf16[32,16,128]{2,1,0:T(8,128)(2,1)}), bf16[32,16,128]{2,1,0:T(8,128)(2,1)S(1)}, u32[]{:S(2)}, u32[]{:S(2)}) %all-to-all-start) | async-done | bytes 131104 | tf_op jit(solution)/shard_map/all_to_all | solution.py:205
  30.8 0.0 copy-start.1
  30.8 0.7 copy-done.1
  31.4 2.1 %harmonic.3 = (bf16[32,24,128]{2,1,0:T(8,128)(2,1)}, f32[8,128]{1,0:T(8,128)}) custom-call(bf16[32,16,128]{2,1,0:T(8,128)(2,1)} %copy-done.1, f32[576,64]{1,0:T(8,128)} %bitcast.7), custom_call_target="tpu_custom_call" | custom-call | tf_op jit(solution)/shard_map/harmonic/pallas_call | solution.py:215
  33.5 12.2 %all_to_all.35.refs_0_ = bf16[32,24,128]{2,1,0:T(8,128)(2,1)} all-to-all(bf16[32,24,128]{2,1,0:T(8,128)(2,1)} %get-tuple-element.19), channel_id=1, replica_groups=mesh['lat'=8,'rad'=4] {'lat','rad'}, dimensions={0} | all-to-all | bytes 393216 | tf_op jit(solution)/shard_map/all_to_all | solution.py:205
  45.8 5.2 %middle.2 = (f32[24,768]{1,0:T(8,128)}, bf16[32,16,128]{2,1,0:T(8,128)(2,1)}) custom-call(bf16[32,24,128]{2,1,0:T(8,128)(2,1)} %all_to_all.35.refs_0_, f32[24,768]{1,0:T(8,128)} %get-tuple-element.20.refs_1_, f32[24,768]{1,0:T(8,128)} %get-tuple-element.21.refs_2_, f32[24,768]{1,0:T(8,128)} %get-tuple-element.22.refs_3_, f32[16,768]{1,0:T(8,128)} %refs_4_.6, ...), custom_call_target="tpu_custom_call" | custom-call | tf_op jit(solution)/shard_map/middle/pallas_call | solution.py:224
  51.0 11.5 %all_to_all.36.refs_0_ = bf16[32,16,128]{2,1,0:T(8,128)(2,1)} all-to-all(bf16[32,16,128]{2,1,0:T(8,128)(2,1)} %get-tuple-element.24), channel_id=1, replica_groups=mesh['lat'=8,'rad'=4] {'lat','rad'}, dimensions={0} | all-to-all | bytes 262144 | tf_op jit(solution)/shard_map/all_to_all | solution.py:205
  62.4 2.1 %harmonic.4 = (bf16[32,24,128]{2,1,0:T(8,128)(2,1)}, f32[8,128]{1,0:T(8,128)}) custom-call(bf16[32,16,128]{2,1,0:T(8,128)(2,1)} %all_to_all.36.refs_0_, f32[576,64]{1,0:T(8,128)} %bitcast.8), custom_call_target="tpu_custom_call" | custom-call | tf_op jit(solution)/shard_map/harmonic/pallas_call | solution.py:215
  64.6 12.2 %all_to_all.37.refs_0_ = bf16[32,24,128]{2,1,0:T(8,128)(2,1)} all-to-all(bf16[32,24,128]{2,1,0:T(8,128)(2,1)} %get-tuple-element.25), channel_id=1, replica_groups=mesh['lat'=8,'rad'=4] {'lat','rad'}, dimensions={0} | all-to-all | bytes 393216 | tf_op jit(solution)/shard_map/all_to_all | solution.py:205
  76.8 5.2 %middle.3 = (f32[24,768]{1,0:T(8,128)}, bf16[32,16,128]{2,1,0:T(8,128)(2,1)}) custom-call(bf16[32,24,128]{2,1,0:T(8,128)(2,1)} %all_to_all.37.refs_0_, f32[24,768]{1,0:T(8,128)} %get-tuple-element.26.refs_1_, f32[24,768]{1,0:T(8,128)} %get-tuple-element.21.refs_2_, f32[24,768]{1,0:T(8,128)} %get-tuple-element.22.refs_3_, f32[16,768]{1,0:T(8,128)} %refs_4_.6, ...), custom_call_target="tpu_custom_call" | custom-call | tf_op jit(solution)/shard_map/middle/pallas_call | solution.py:224
  82.0 11.4 %all_to_all.38.refs_0_ = bf16[32,16,128]{2,1,0:T(8,128)(2,1)} all-to-all(bf16[32,16,128]{2,1,0:T(8,128)(2,1)} %get-tuple-element.27), channel_id=1, replica_groups=mesh['lat'=8,'rad'=4] {'lat','rad'}, dimensions={0} | all-to-all | bytes 262144 | tf_op jit(solution)/shard_map/all_to_all | solution.py:205
  93.4 2.1 %harmonic.5 = (bf16[32,24,128]{2,1,0:T(8,128)(2,1)}, f32[8,128]{1,0:T(8,128)}) custom-call(bf16[32,16,128]{2,1,0:T(8,128)(2,1)} %all_to_all.38.refs_0_, f32[576,64]{1,0:T(8,128)} %bitcast.9), custom_call_target="tpu_custom_call" | custom-call | tf_op jit(solution)/shard_map/harmonic/pallas_call | solution.py:215
  95.6 12.2 %all_to_all.39.refs_0_ = bf16[32,24,128]{2,1,0:T(8,128)(2,1)} all-to-all(bf16[32,24,128]{2,1,0:T(8,128)(2,1)} %get-tuple-element.28), channel_id=1, replica_groups=mesh['lat'=8,'rad'=4] {'lat','rad'}, dimensions={0} | all-to-all | bytes 393216 | tf_op jit(solution)/shard_map/all_to_all | solution.py:205
  107.8 4.1 %last.1 = (f32[16,768]{1,0:T(8,128)}, f32[32,1,128]{2,1,0:T(1,128)}) custom-call(bf16[32,24,128]{2,1,0:T(8,128)(2,1)} %all_to_all.39.refs_0_, f32[24,768]{1,0:T(8,128)} %get-tuple-element.29.refs_1_, f32[24,768]{1,0:T(8,128)} %get-tuple-element.21.refs_2_, f32[24,768]{1,0:T(8,128)} %get-tuple-element.22.refs_3_, bf16[2408,768]{1,0:T(8,128)(2,1)} %refs_4_.7, ...), custom_call_target="tpu_custom_call" | custom-call | tf_op jit(solution)/shard_map/last/pallas_call | solution.py:228
  111.9 2.6 %all-to-all-start.6 = ((f32[32,1,128]{2,1,0:T(1,128)}), f32[32,1,128]{2,1,0:T(1,128)S(1)}, u32[]{:S(2)}, u32[]{:S(2)}) async-start(f32[32,1,128]{2,1,0:T(1,128)} %get-tuple-element.33), calls=%async_computation.6 | async-start | bytes 32768 | tf_op jit(solution)/shard_map/all_to_all | solution.py:205
  114.5 1.2 slice.33
  115.7 1.2 slice.34
  116.8 4.8 %all-to-all-done.6 = f32[32,1,128]{2,1,0:T(1,128)S(1)} async-done(((f32[32,1,128]{2,1,0:T(1,128)}), f32[32,1,128]{2,1,0:T(1,128)S(1)}, u32[]{:S(2)}, u32[]{:S(2)}) %all-to-all-start.6) | async-done | bytes 16416 | tf_op jit(solution)/shard_map/all_to_all | solution.py:205
  121.7 0.7 slice_reduce_fusion
  122.4 2.4 %fusion = f32[3]{0:T(128)} fusion(f32[1]{0:T(128)} %bitcast.6, f32[1]{0:T(128)} %bitcast.5, f32[1]{0:T(128)} %bitcast.4), kind=kLoop, calls=%fused_computation.5 | loop fusion | flops 9 | bytes 24 | tf_op jit(solution)/shard_map/sqrt | solution.py:235
  (2 shorter events, 0.0 us)
Async XLA Ops:
  0.6 22.2 %copy-start = (f32[49,64,64]{2,1,0:T(8,128)S(1)}, f32[49,64,64]{2,1,0:T(8,128)}, u32[]{:S(2)}) copy-start(f32[49,64,64]{2,1,0:T(8,128)} %param.15) | copy-start | bytes 2408452
  2.4 5.1 %collective-permute-start.1 = (f32[3,768]{1,0:T(4,128)S(1)}, f32[3,768]{1,0:T(4,128)S(1)}, u32[]{:S(2)}, u32[]{:S(2)}) collective-permute-start(f32[3,768]{1,0:T(4,128)S(1)} %pad_maximum_fusion.2), channel_id=1, source_target_pairs={{0,1},{1,2},{2,3},{4,5},{5,6},{6,7},{8,9},{9,10},{10,11},{12,13},{... | collective-permute-start | bytes 27656 | tf_op jit(solution)/shard_map/ppermute | solution.py:186
  4.8 5.2 %collective-permute-start = (f32[3,768]{1,0:T(4,128)S(1)}, f32[3,768]{1,0:T(4,128)S(1)}, u32[]{:S(2)}, u32[]{:S(2)}) collective-permute-start(f32[3,768]{1,0:T(4,128)S(1)} %pad_maximum_fusion.1), channel_id=1, source_target_pairs={{1,0},{2,1},{3,2},{5,4},{6,5},{7,6},{9,8},{10,9},{11,10},{13,12},{... | collective-permute-start | bytes 27656 | tf_op jit(solution)/shard_map/ppermute | solution.py:187
  15.6 15.2 %all-to-all-start = ((bf16[32,16,128]{2,1,0:T(8,128)(2,1)}), bf16[32,16,128]{2,1,0:T(8,128)(2,1)S(1)}, u32[]{:S(2)}, u32[]{:S(2)}) async-start(bf16[32,16,128]{2,1,0:T(8,128)(2,1)} %get-tuple-element.18), calls=%async_computation | async-start | bytes 262144 | tf_op jit(solution)/shard_map/all_to_all | solution.py:205
  30.8 0.7 copy-start.1
  111.9 9.7 %all-to-all-start.6 = ((f32[32,1,128]{2,1,0:T(1,128)}), f32[32,1,128]{2,1,0:T(1,128)S(1)}, u32[]{:S(2)}, u32[]{:S(2)}) async-start(f32[32,1,128]{2,1,0:T(1,128)} %get-tuple-element.33), calls=%async_computation.6 | async-start | bytes 32768 | tf_op jit(solution)/shard_map/all_to_all | solution.py:205

commit v2 on v1

v2 whole, which is shorter than its diff:
```python
import jax
import jax.numpy as jnp
from jax import lax
from jax.experimental import pallas as pl
from jax.experimental.pallas import tpu as pltpu
from jax.sharding import PartitionSpec as P

DEG = 48
L = 64
ITERS = 3
LANES = 128
TAIL = 8
VMEM_LIMIT = 16 << 20
GROUP = 4

F32, BF16 = jnp.float32, jnp.bfloat16
NT = (((1,), (1,)), ((), ()))
NN = (((1,), (0,)), ((), ()))


def degree_of(k):
    d = 0
    while (d + 1) * (d + 1) <= k:
        d += 1
    return d


def chunks_of(slots, chunk):
    return [(k, min(k + chunk, slots)) for k in range(0, slots, chunk)]


def bf16_parts(x, count):
    parts = []
    for _ in range(count):
        part = x.astype(BF16)
        parts.append(part)
        x = x - part.astype(F32)
    return parts


def build_counts(nb_ref, counts_ref):
    tile = counts_ref.shape[1]
    rows = 32

    def body(b, carry):
        at = pl.multiple_of(b * rows, rows)
        source = lax.broadcasted_iota(jnp.int32, (rows, tile), 0) + at
        total = jnp.zeros((rows, tile), F32)
        for j in range(nb_ref.shape[0]):
            total = total + (source == nb_ref[j : j + 1, :]).astype(F32)
        counts_ref[pl.ds(at, rows), :] = total.astype(BF16)
        return carry

    lax.fori_loop(0, tile // rows, body, 0)


def column(row_ref, rows):
    square = (rows, rows)
    same = lax.broadcasted_iota(jnp.int32, square, 0) == lax.broadcasted_iota(jnp.int32, square, 1)
    spread = jnp.broadcast_to(row_ref[...], square)
    return jnp.sum(jnp.where(same, spread, 0.0), axis=1, keepdims=True)


def analyse(u, grad_ref, dens_ref, basis_ref, send_ref, squares, chunk, ready=lambda d: None):
    own, columns = u.shape
    row = lax.broadcasted_iota(jnp.int32, u.shape, 0)
    above = jnp.where(row == own - 1, 0.0, pltpu.roll(u, own - 1, 0))
    below = jnp.where(row == 0, 0.0, pltpu.roll(u, 1, 0))
    rho = grad_ref[...] * u + column(dens_ref, own) * ((above - below) * 0.5)
    side = lax.broadcasted_iota(jnp.int32, (TAIL, columns), 0) % 2
    edges = jnp.where(side == 0, u[:1], u[own - 1 :])
    rows = jnp.concatenate([rho, edges], axis=0).astype(BF16)

    lane = lax.broadcasted_iota(jnp.int32, (own, LANES), 1)
    row = lax.broadcasted_iota(jnp.int32, (own, LANES), 0)
    rest = jnp.zeros((own, LANES), F32)
    values = [dens_ref[:, 0:1], dens_ref[:, own - 1 : own]]
    if squares is not None:
        values.append(squares)
    for n, value in enumerate(values):
        for m, part in enumerate(bf16_parts(value, 3)):
            rest = jnp.where((row == 4 + n) & (lane == chunk + m), part.astype(F32), rest)
    room = LANES - chunk
    low = lax.broadcasted_iota(jnp.int32, (TAIL, LANES), 0)
    pieces = chunks_of(basis_ref.shape[0], chunk)
    for d in range(len(pieces), send_ref.shape[0]):
        send_ref[d] = rest.astype(BF16)
    for d, (start, end) in enumerate(pieces):
        ready(d)
        part = lax.dot_general(rows, basis_ref[start:end, :], NT, preferred_element_type=F32)
        if end - start < LANES:
            part = jnp.concatenate(
                [part, jnp.zeros((own + TAIL, LANES - (end - start)), F32)], axis=1
            )
        sides = part[own:]
        moved = pltpu.roll(sides, chunk, 1)
        if chunk > room:
            moved = jnp.where(low < 2, moved, pltpu.roll(sides, chunk - room, 1))
        moved = jnp.where(low < 4, moved, rest[:TAIL])
        moved = jnp.concatenate([moved, rest[TAIL:]], axis=0)
        send_ref[d] = jnp.where(lane < chunk, part[:own], moved).astype(BF16)


def total_of(x):
    return jnp.sum(jnp.sum(x, axis=0, keepdims=True), axis=1, keepdims=True)


def advance(recv_ref, change_ref, u_ref, rate_ref, basis_ref, chunk):
    force = jnp.zeros(u_ref.shape, F32)
    for d, (start, end) in enumerate(chunks_of(basis_ref.shape[0], chunk)):
        force = force + lax.dot_general(
            recv_ref[d][:, 0 : end - start], basis_ref[start:end, :], NN, preferred_element_type=F32
        )
    change = change_ref[...] + rate_ref[...] * force
    return u_ref[...] + change, total_of(change * change)


def lateral(u, load, rate, counts):
    rows = u.shape[0]
    parts = jnp.concatenate(bf16_parts(u, 3), axis=0)
    sums = lax.dot_general(parts, counts[...], NN, preferred_element_type=F32)
    lap = sums[:rows] + sums[rows : 2 * rows] + sums[2 * rows :] - 4.0 * u
    return rate[...] * (load[...] + lap - u)


def first_kernel(chunk, lows, *refs):
    sources, (counts, change, send, sems) = refs[:8], refs[16:]
    targets = refs[8:16]
    u, load, grad, rate, dens, nb, mine, basis = targets
    green = sources[6]
    device = lax.axis_index("lat") * lax.axis_size("rad") + lax.axis_index("rad")
    copies = []
    slots = basis.shape[0]
    for source, target in zip(sources[:6], targets[:6]):
        copies.append((source, target))
    copies.append((green.at[pl.ds(lows(device), mine.shape[0])], mine))
    groups = chunks_of(slots, GROUP * chunk)
    for start, end in groups:
        copies.append((sources[7].at[start:end], basis.at[start:end]))
    order = [5, 0, 2, 4] + list(range(7, len(copies))) + [1, 3, 6]
    copies = [pltpu.make_async_copy(*c, sems.at[n]) for n, c in enumerate(copies)]
    for n in order:
        copies[n].start()
    copies[5].wait()
    build_counts(nb, counts)
    for n in (0, 2, 4):
        copies[n].wait()

    def ready(d):
        if d % GROUP == 0:
            copies[7 + d // GROUP].wait()

    analyse(u[...], grad, dens, basis, send, None, chunk, ready)
    for n in (1, 3, 6):
        copies[n].wait()
    change[...] = lateral(u[...], load, rate, counts)


def middle_kernel(chunk, recv, change, u, load, rate, grad, dens, basis, counts, u_out, send, later):
    new, squares = advance(recv, change, u, rate, basis, chunk)
    u_out[...] = new
    analyse(new, grad, dens, basis, send, squares, chunk)
    later[...] = lateral(new, load, rate, counts)


def last_kernel(chunk, recv, change, u, rate, basis, relaxed, send):
    new, squares = advance(recv, change, u, rate, basis, chunk)
    relaxed[...] = new
    send[...] = jnp.broadcast_to(squares.reshape(1, 1, 1), send.shape)


def harmonic_kernel(lats, rads, chunk, degrees, lows, recv, green, send, total):
    own = recv.shape[1]
    layers = rads * own
    room = LANES - chunk
    device = lax.axis_index("lat") * rads + lax.axis_index("rad")
    blocks, tops, bottoms, squares = [], [], [], 0.0
    low = lax.broadcasted_iota(jnp.int32, (TAIL, LANES), 0)
    at = lax.broadcasted_iota(jnp.int32, (TAIL, LANES), 1)

    def value(tile, n):
        return total_of(jnp.where((low == 4 + n) & (at >= chunk), tile, 0.0))

    for j in range(rads):
        block = recv[j].astype(F32)
        for i in range(1, lats):
            block = block + recv[i * rads + j].astype(F32)
        tile = block[:TAIL]
        sides = pltpu.roll(tile, room, 1)
        if chunk > room:
            other = pltpu.roll(pltpu.roll(tile, TAIL - 2, 0), 2 * room, 1)
            sides = jnp.where(at < room, sides, other)
        blocks.append(block)
        tops.append(sides[0:1])
        bottoms.append(sides[1:2])
        squares = squares + value(tile, 2)
    total[...] = jnp.broadcast_to(squares, total.shape)
    row = lax.broadcasted_iota(jnp.int32, (own, LANES), 0)
    for j in range(rads):
        block, tile = blocks[j], blocks[j][:TAIL]
        if j > 0:
            edge = (value(tile, 0) * (0.5 / lats)) * bottoms[j - 1]
            block = block - jnp.where(row == 0, edge, 0.0)
        if j < rads - 1:
            edge = (value(tile, 1) * (0.5 / lats)) * tops[j + 1]
            block = block + jnp.where(row == own - 1, edge, 0.0)
        blocks[j] = block
    coefs = jnp.concatenate(blocks, axis=0)
    every = lax.dot_general(
        green[...].reshape(degrees * layers, layers), coefs, NN, precision=lax.Precision.HIGHEST, preferred_element_type=F32
    )
    lane = lax.broadcasted_iota(jnp.int32, (layers, LANES), 1)
    row = lax.broadcasted_iota(jnp.int32, (layers, LANES), 0)
    k = lane + device * chunk
    start = lows(device)
    phi = jnp.zeros((layers, LANES), F32)
    for n in range(degrees):
        degree = start + n
        mine = (k >= degree * degree) & (k < (degree + 1) * (degree + 1)) & (lane < chunk)
        phi = jnp.where(mine, every[n * layers : (n + 1) * layers], phi)
    above = jnp.where(row == layers - 1, 0.0, pltpu.roll(phi, layers - 1, 0))
    below = jnp.where(row == 0, 0.0, pltpu.roll(phi, 1, 0))
    step = ((above - below) * 0.5).astype(BF16)
    for j in range(rads):
        for i in range(lats):
            send[i * rads + j] = step[j * own : (j + 1) * own]


def final_kernel(recv, one, two, sizes, *, nodes):
    last = jnp.sum(recv[...], axis=0)[:, 0:1]
    for n, total in enumerate((one[0:1, 0:1], two[0:1, 0:1], last)):
        sizes[n] = jnp.sqrt(total / nodes)[0, 0]


def local(displacement, surface_load, dens_grad, dens_ref, relax_rate, basis, neighbours, green):
    own, columns = displacement.shape
    slots = basis.shape[0]
    lats, rads = lax.axis_size("lat"), lax.axis_size("rad")
    devices = lats * rads
    both = ("lat", "rad")
    chunk = -(-slots // devices)
    chunk = -(-chunk // 16) * 16
    layers = rads * own
    firsts = [min(degree_of(k), DEG) for k in range(0, devices * chunk, chunk)]
    lasts = [min(degree_of(k + chunk - 1), DEG) for k in range(0, devices * chunk, chunk)]
    degrees = max(b - a + 1 for a, b in zip(firsts, lasts))

    def lows(device):
        k = device * chunk
        count = jnp.int32(0)
        for d in range(1, DEG + 1):
            count = count + (k >= d * d).astype(jnp.int32)
        return jnp.minimum(count, DEG + 1 - degrees)

    dens = dens_ref.reshape(1, own)
    field = pltpu.VMEM((own, columns), F32)
    packet = pltpu.VMEM((devices, own, LANES), BF16)

    def call(name, kernel, args, out_shape, **more):
        def body(*refs):
            kernel(*args, *refs)

        return pl.pallas_call(
            body,
            out_shape=out_shape,
            name=name,
            compiler_params=pltpu.CompilerParams(vmem_limit_bytes=VMEM_LIMIT),
            **more,
        )

    def exchange(x):
        return lax.all_to_all(x, both, 0, 0, tiled=True)

    groups = len(chunks_of(slots, GROUP * chunk))
    u, load, grad, rate, dens, _, mine, basis, counts, change, send = call(
        "first",
        first_kernel,
        (chunk, lows),
        (
            field,
            field,
            field,
            field,
            pltpu.VMEM((1, own), F32),
            pltpu.VMEM(neighbours.shape, jnp.int32),
            pltpu.VMEM((degrees, L, L), F32),
            pltpu.VMEM(basis.shape, BF16),
            pltpu.VMEM((columns, columns), BF16),
            field,
            packet,
        ),
        in_specs=[pl.BlockSpec(memory_space=pltpu.HBM)] * 8,
        scratch_shapes=[pltpu.SemaphoreType.DMA((7 + groups,))],
    )(
        *(
            pltpu.with_memory_space_constraint(x, pltpu.HBM)
            for x in (
                displacement, surface_load, dens_grad, relax_rate, dens, neighbours, green, basis
            )
        )
    )
    totals = []
    for it in range(ITERS):
        send, total = call(
            "harmonic",
            harmonic_kernel,
            (lats, rads, chunk, degrees, lows),
            (packet, pltpu.VMEM((8, LANES), F32)),
        )(exchange(send), mine)
        totals.append(total)
        recv = exchange(send)
        if it < ITERS - 1:
            u, send, change = call("middle", middle_kernel, (chunk,), (field, packet, field))(
                recv, change, u, load, rate, grad, dens, basis, counts
            )
        else:
            relaxed, send = call(
                "last",
                last_kernel,
                (chunk,),
                (
                    jax.ShapeDtypeStruct((own, columns), F32),
                    pltpu.VMEM((devices, 1, LANES), F32),
                ),
            )(recv, change, u, rate, basis)
    nodes = layers * columns * lats
    sizes = call(
        "final",
        lambda *refs: final_kernel(*refs, nodes=nodes),
        (),
        jax.ShapeDtypeStruct((ITERS,), F32),
        out_specs=pl.BlockSpec(memory_space=pltpu.SMEM),
    )(exchange(send), totals[1], totals[2])
    return (relaxed, sizes)


def solution(mesh):
    placed = (
        P("rad", "lat"),
        P("rad", "lat"),
        P("rad", "lat"),
        P("rad"),
        P("rad", "lat"),
        P(None, "lat"),
        P(None, "lat"),
        P(),
    )
    return jax.shard_map(
        local, mesh=mesh, in_specs=placed, out_specs=(P("rad", "lat"), P()), check_vma=False
    )
```

time: 125 us -> 88.8 us (0.71)
  waiting for transfers between devices: 14.6 us -> 0 us
  blocking collectives: 59.5 us -> 74.1 us
  starting transfers between devices: 13.2 us -> 0 us
  Pallas kernels: 26 us -> 13.6 us
  local copies, waits for them, and re-layouts: 6.75 us -> 0 us
  other arithmetic: 3.75 us -> 0 us
    all_to_all x5 -> x7, blocking collectives: 59.5 us -> 74.1 us  [exchange(): return lax.all_to_all(x, both, 0, 0, tiled=True)]
    pallas_call x7 -> x8, Pallas kernels: 26 us -> 13.6 us  [the longest x1 5.25 us: local(): call('first', first_kernel, (chunk, lows), (field, field, field, field, p...]
    all_to_all x2 -> x0, waiting for transfers between devices: 12.1 us -> none  [exchange(): return lax.all_to_all(x, both, 0, 0, tiled=True)]
    all_to_all x2 -> x0, starting transfers between devices: 9.52 us -> none  [exchange(): return lax.all_to_all(x, both, 0, 0, tiled=True)]
    slice x4 -> x0, local copies, waits for them, and re-layouts: 4.02 us -> none  [the longest x2 2.34 us: local(): totals.append(total[0, 0])]
    ppermute x2 -> x0, starting transfers between devices: 3.69 us -> none  [the longest x1 2.4 us: local(): before = lax.ppermute(tops, 'rad', up)]
    ppermute x2 -> x0, waiting for transfers between devices: 2.54 us -> none  [the longest x1 2.54 us: local(): after = lax.ppermute(bottoms, 'rad', down)]
    sqrt x1 -> x0, other arithmetic: 2.39 us -> none  [local(): return (relaxed, jnp.sqrt(sums / (layers * columns * lats)))]
  transfers between devices with their start and end apart: 4 -> 0, of which waited for: 3 -> 0; matrix products, arithmetic and copies ran while one was open for 4% -> 0% of each run, Pallas kernels for 0% -> 0%
where the time goes in v2:
time: 88.8 us; the launch traced here: 88.4 us
  blocking collectives  74.1 us (83%)
  Pallas kernels  13.6 us (15%)
    all_to_all x7, blocking collectives, exchange(): return lax.all_to_all(x, both, 0, 0, tiled=True)  74.1 us
    pallas_call x1, Pallas kernels, local(): call('first', first_kernel, (chunk, lows), (field, field, field, field, p...  5.25 us
    pallas_call x2, Pallas kernels, local(): call('middle', middle_kernel, (chunk,), (field, packet, field))  4.46 us
    pallas_call x3, Pallas kernels, local(): call('harmonic', harmonic_kernel, (lats, rads, chunk, degrees, lows), (pa...  2.08 us

profile of v2, /device:TPU:0, one launch (start us, length us, event | category | flops | bytes accessed | tf_op | source)
XLA Modules:
  0.0 88.4 jit_solution(1115537002879509923)
XLA Ops:
  0.6 5.2 %first.1 = (f32[16,768]{1,0:T(8,128)S(1)}, f32[16,768]{1,0:T(8,128)S(1)}, f32[16,768]{1,0:T(8,128)S(1)}, f32[16,768]{1,0:T(8,128)S(1)}, f32[1,16]{1,0:T(1,128)S(...) custom-call(f32[16,768]{1,0:T(8,128)} %refs_0_.1, ...), custom_call_target="tpu_custom_call" | custom-call | tf_op jit(solution)/shard_map/first/pallas_call | solution.py:275
  5.9 15.3 %all_to_all.35.refs_0_ = bf16[32,16,128]{2,1,0:T(8,128)(2,1)S(1)} all-to-all(bf16[32,16,128]{2,1,0:T(8,128)(2,1)S(1)} %get-tuple-element.25), channel_id=1, replica_groups=mesh['lat'=8,'rad'=4] {'lat','rad'}, dimensions={0} | all-to-all | bytes 262144 | tf_op jit(solution)/shard_map/all_to_all | solution.py:272
  21.2 1.0 %harmonic.3 = (bf16[32,16,128]{2,1,0:T(8,128)(2,1)S(1)}, f32[8,128]{1,0:T(8,128)}) custom-call(bf16[32,16,128]{2,1,0:T(8,128)(2,1)S(1)} %all_to_all.35.refs_0_, f32[9,64,64]{2,1,0:T(8,128)S(1)} %get-tuple-element.26.refs_1_), custom_call_target="tpu_custom_call" | custom-call | tf_op jit(solution)/shard_map/harmonic/pallas_call | solution.py:304
  22.3 10.0 %all_to_all.36.refs_0_ = bf16[32,16,128]{2,1,0:T(8,128)(2,1)S(1)} all-to-all(bf16[32,16,128]{2,1,0:T(8,128)(2,1)S(1)} %get-tuple-element.27), channel_id=1, replica_groups=mesh['lat'=8,'rad'=4] {'lat','rad'}, dimensions={0} | all-to-all | bytes 262144 | tf_op jit(solution)/shard_map/all_to_all | solution.py:272
  32.2 2.2 %middle.2 = (f32[16,768]{1,0:T(8,128)S(1)}, bf16[32,16,128]{2,1,0:T(8,128)(2,1)S(1)}, f32[16,768]{1,0:T(8,128)S(1)}) custom-call(bf16[32,16,128]{2,1,0:T(8,128)(2,1)S(1)} %all_to_all.36.refs_0_, f32[16,768]{1,0:T(8,128)S(1)} %get-tuple-element.28.refs_1_, f32[16,768]{1,0:T(8,128)S(1)} %get-tuple-element.29.refs_2_, f32[16,768]{1,0:T(8,128)S(1)} %get-tuple-element.30.refs_3_, ...), custom_call_target="tpu_custom_call" | custom-call | tf_op jit(solution)/shard_map/middle/pallas_call | solution.py:313
  34.5 10.0 %all_to_all.37.refs_0_ = bf16[32,16,128]{2,1,0:T(8,128)(2,1)S(1)} all-to-all(bf16[32,16,128]{2,1,0:T(8,128)(2,1)S(1)} %get-tuple-element.36), channel_id=1, replica_groups=mesh['lat'=8,'rad'=4] {'lat','rad'}, dimensions={0} | all-to-all | bytes 262144 | tf_op jit(solution)/shard_map/all_to_all | solution.py:272
  44.4 0.5 harmonic.4
  45.0 10.0 %all_to_all.38.refs_0_ = bf16[32,16,128]{2,1,0:T(8,128)(2,1)S(1)} all-to-all(bf16[32,16,128]{2,1,0:T(8,128)(2,1)S(1)} %get-tuple-element.37), channel_id=1, replica_groups=mesh['lat'=8,'rad'=4] {'lat','rad'}, dimensions={0} | all-to-all | bytes 262144 | tf_op jit(solution)/shard_map/all_to_all | solution.py:272
  54.9 2.2 %middle.3 = (f32[16,768]{1,0:T(8,128)S(1)}, bf16[32,16,128]{2,1,0:T(8,128)(2,1)S(1)}, f32[16,768]{1,0:T(8,128)S(1)}) custom-call(bf16[32,16,128]{2,1,0:T(8,128)(2,1)S(1)} %all_to_all.38.refs_0_, f32[16,768]{1,0:T(8,128)S(1)} %get-tuple-element.38.refs_1_, f32[16,768]{1,0:T(8,128)S(1)} %get-tuple-element.39.refs_2_, f32[16,768]{1,0:T(8,128)S(1)} %get-tuple-element.30.refs_3_, ...), custom_call_target="tpu_custom_call" | custom-call | tf_op jit(solution)/shard_map/middle/pallas_call | solution.py:313
  57.2 10.0 %all_to_all.39.refs_0_ = bf16[32,16,128]{2,1,0:T(8,128)(2,1)S(1)} all-to-all(bf16[32,16,128]{2,1,0:T(8,128)(2,1)S(1)} %get-tuple-element.40), channel_id=1, replica_groups=mesh['lat'=8,'rad'=4] {'lat','rad'}, dimensions={0} | all-to-all | bytes 262144 | tf_op jit(solution)/shard_map/all_to_all | solution.py:272
  67.1 0.5 harmonic.5
  67.7 10.0 %all_to_all.40.refs_0_ = bf16[32,16,128]{2,1,0:T(8,128)(2,1)S(1)} all-to-all(bf16[32,16,128]{2,1,0:T(8,128)(2,1)S(1)} %get-tuple-element.41), channel_id=1, replica_groups=mesh['lat'=8,'rad'=4] {'lat','rad'}, dimensions={0} | all-to-all | bytes 262144 | tf_op jit(solution)/shard_map/all_to_all | solution.py:272
  77.6 1.2 %last.1 = (f32[16,768]{1,0:T(8,128)}, f32[32,1,128]{2,1,0:T(1,128)S(1)}) custom-call(bf16[32,16,128]{2,1,0:T(8,128)(2,1)S(1)} %all_to_all.40.refs_0_, f32[16,768]{1,0:T(8,128)S(1)} %get-tuple-element.42.refs_1_, f32[16,768]{1,0:T(8,128)S(1)} %get-tuple-element.43.refs_2_, f32[16,768]{1,0:T(8,128)S(1)} %get-tuple-element.31.refs_4_.refs_3_, ...), custom_call_target="tpu_custom_call" | custom-call | tf_op jit(solution)/shard_map/last/pallas_call | solution.py:317
  78.9 8.9 %all_to_all.41.refs_0_ = f32[32,1,128]{2,1,0:T(1,128)S(1)} all-to-all(f32[32,1,128]{2,1,0:T(1,128)S(1)} %get-tuple-element.45), channel_id=1, replica_groups=mesh['lat'=8,'rad'=4] {'lat','rad'}, dimensions={0} | all-to-all | bytes 32768 | tf_op jit(solution)/shard_map/all_to_all | solution.py:272
  87.8 0.6 final.1

commit v3 on v2

--- a/solution.py
+++ b/solution.py
@@ -9,9 +9,10 @@
 L = 64
 ITERS = 3
 LANES = 128
-TAIL = 8
+TILE = 8
+QUARTER = 4
 VMEM_LIMIT = 16 << 20
-GROUP = 4
+GROUP = 16
 
 F32, BF16 = jnp.float32, jnp.bfloat16
 NT = (((1,), (1,)), ((), ()))
@@ -67,38 +68,65 @@
     above = jnp.where(row == own - 1, 0.0, pltpu.roll(u, own - 1, 0))
     below = jnp.where(row == 0, 0.0, pltpu.roll(u, 1, 0))
     rho = grad_ref[...] * u + column(dens_ref, own) * ((above - below) * 0.5)
-    side = lax.broadcasted_iota(jnp.int32, (TAIL, columns), 0) % 2
+    side = lax.broadcasted_iota(jnp.int32, (TILE, columns), 0) % 2
     edges = jnp.where(side == 0, u[:1], u[own - 1 :])
-    rows = jnp.concatenate([rho, edges], axis=0).astype(BF16)
-
-    lane = lax.broadcasted_iota(jnp.int32, (own, LANES), 1)
-    row = lax.broadcasted_iota(jnp.int32, (own, LANES), 0)
-    rest = jnp.zeros((own, LANES), F32)
+    third, over = rho[TILE : TILE + QUARTER], rho[TILE + QUARTER :]
+    rows = [rho[:TILE], third, third, over, over, edges]
+    rows = jnp.concatenate(rows, axis=0).astype(BF16)
+
+    room, spare = spaces(chunk)
+    at = lax.broadcasted_iota(jnp.int32, (TILE, LANES), 1)
+    low = lax.broadcasted_iota(jnp.int32, (TILE, LANES), 0)
+    rest = jnp.zeros((TILE, LANES), F32)
     values = [dens_ref[:, 0:1], dens_ref[:, own - 1 : own]]
     if squares is not None:
         values.append(squares)
     for n, value in enumerate(values):
         for m, part in enumerate(bf16_parts(value, 3)):
-            rest = jnp.where((row == 4 + n) & (lane == chunk + m), part.astype(F32), rest)
-    room = LANES - chunk
-    low = lax.broadcasted_iota(jnp.int32, (TAIL, LANES), 0)
+            rest = jnp.where((low == QUARTER + n) & (at == spare + m), part.astype(F32), rest)
     pieces = chunks_of(basis_ref.shape[0], chunk)
     for d in range(len(pieces), send_ref.shape[0]):
-        send_ref[d] = rest.astype(BF16)
+        store(send_ref, d, rest, jnp.zeros((TILE, LANES), F32))
     for d, (start, end) in enumerate(pieces):
         ready(d)
         part = lax.dot_general(rows, basis_ref[start:end, :], NT, preferred_element_type=F32)
         if end - start < LANES:
             part = jnp.concatenate(
-                [part, jnp.zeros((own + TAIL, LANES - (end - start)), F32)], axis=1
+                [part, jnp.zeros((4 * TILE, LANES - (end - start)), F32)], axis=1
             )
-        sides = part[own:]
-        moved = pltpu.roll(sides, chunk, 1)
-        if chunk > room:
-            moved = jnp.where(low < 2, moved, pltpu.roll(sides, chunk - room, 1))
-        moved = jnp.where(low < 4, moved, rest[:TAIL])
-        moved = jnp.concatenate([moved, rest[TAIL:]], axis=0)
-        send_ref[d] = jnp.where(lane < chunk, part[:own], moved).astype(BF16)
+        main, more, over, sides = [part[n : n + TILE] for n in range(0, 4 * TILE, TILE)]
+        over, sides = [
+            jnp.where(low < split, pltpu.roll(x, chunk, 1), behind(x, chunk))
+            for x, split in ((over, QUARTER), (sides, 2))
+        ]
+        over = jnp.where((at >= spare) & (low >= QUARTER), rest, over)
+        main = jnp.where(at < chunk, main, over)
+        store(send_ref, d, main, jnp.where(at < chunk, more, sides))
+
+
+def spaces(chunk):
+    room = LANES - chunk
+    return room, chunk + max(0, chunk - room)
+
+
+def behind(x, chunk):
+    room, _ = spaces(chunk)
+    return pltpu.roll(x, chunk - room, 1) if chunk > room else jnp.zeros_like(x)
+
+
+def store(ref, d, main, more):
+    ref[d, 0] = main[:QUARTER].astype(BF16)
+    ref[d, 1] = main[QUARTER:].astype(BF16)
+    ref[d, 2] = more[:QUARTER].astype(BF16)
+
+
+def unfolded(one, two, chunk):
+    room, _ = spaces(chunk)
+    first = pltpu.roll(one, room, 1)
+    if chunk <= room:
+        return first
+    at = lax.broadcasted_iota(jnp.int32, one.shape, 1)
+    return jnp.where(at < room, first, pltpu.roll(two, 2 * room, 1))
 
 
 def total_of(x):
@@ -108,8 +136,13 @@
 def advance(recv_ref, change_ref, u_ref, rate_ref, basis_ref, chunk):
     force = jnp.zeros(u_ref.shape, F32)
     for d, (start, end) in enumerate(chunks_of(basis_ref.shape[0], chunk)):
+        packet = [recv_ref[d, n].astype(F32) for n in range(3)]
+        packet = jnp.concatenate(packet + [unfolded(packet[0], packet[1], chunk)], axis=0)
         force = force + lax.dot_general(
-            recv_ref[d][:, 0 : end - start], basis_ref[start:end, :], NN, preferred_element_type=F32
+            packet.astype(BF16)[:, 0 : end - start],
+            basis_ref[start:end, :],
+            NN,
+            preferred_element_type=F32,
         )
     change = change_ref[...] + rate_ref[...] * force
     return u_ref[...] + change, total_of(change * change)
@@ -169,42 +202,41 @@
     send[...] = jnp.broadcast_to(squares.reshape(1, 1, 1), send.shape)
 
 
-def harmonic_kernel(lats, rads, chunk, degrees, lows, recv, green, send, total):
-    own = recv.shape[1]
+def harmonic_kernel(lats, rads, chunk, degrees, lows, recv, green, send, *total):
+    own = 4 * QUARTER
     layers = rads * own
-    room = LANES - chunk
+    _, spare = spaces(chunk)
     device = lax.axis_index("lat") * rads + lax.axis_index("rad")
-    blocks, tops, bottoms, squares = [], [], [], 0.0
-    low = lax.broadcasted_iota(jnp.int32, (TAIL, LANES), 0)
-    at = lax.broadcasted_iota(jnp.int32, (TAIL, LANES), 1)
+    low = lax.broadcasted_iota(jnp.int32, (QUARTER, LANES), 0)
+    at = lax.broadcasted_iota(jnp.int32, (QUARTER, LANES), 1)
+    packets, tops, bottoms, squares = [], [], [], 0.0
 
     def value(tile, n):
-        return total_of(jnp.where((low == 4 + n) & (at >= chunk), tile, 0.0))
+        return total_of(jnp.where((low == n) & (at >= spare), tile, 0.0))
 
     for j in range(rads):
-        block = recv[j].astype(F32)
+        packet = [recv[j, n].astype(F32) for n in range(3)]
         for i in range(1, lats):
-            block = block + recv[i * rads + j].astype(F32)
-        tile = block[:TAIL]
-        sides = pltpu.roll(tile, room, 1)
-        if chunk > room:
-            other = pltpu.roll(pltpu.roll(tile, TAIL - 2, 0), 2 * room, 1)
-            sides = jnp.where(at < room, sides, other)
-        blocks.append(block)
-        tops.append(sides[0:1])
-        bottoms.append(sides[1:2])
-        squares = squares + value(tile, 2)
-    total[...] = jnp.broadcast_to(squares, total.shape)
+            packet = [x + recv[i * rads + j, n].astype(F32) for n, x in enumerate(packet)]
+        packets.append(packet)
+        sides = [packet[2][n : n + 1] for n in range(4)]
+        tops.append(unfolded(sides[0], sides[2], chunk))
+        bottoms.append(unfolded(sides[1], sides[3], chunk))
+        if total:
+            squares = squares + value(packet[1], 2)
+    if total:
+        total[0][...] = jnp.broadcast_to(squares, total[0].shape)
     row = lax.broadcasted_iota(jnp.int32, (own, LANES), 0)
-    for j in range(rads):
-        block, tile = blocks[j], blocks[j][:TAIL]
+    blocks = []
+    for j, packet in enumerate(packets):
+        block = jnp.concatenate(packet + [unfolded(packet[0], packet[1], chunk)], axis=0)
         if j > 0:
-            edge = (value(tile, 0) * (0.5 / lats)) * bottoms[j - 1]
+            edge = (value(packet[1], 0) * (0.5 / lats)) * bottoms[j - 1]
             block = block - jnp.where(row == 0, edge, 0.0)
         if j < rads - 1:
-            edge = (value(tile, 1) * (0.5 / lats)) * tops[j + 1]
+            edge = (value(packet[1], 1) * (0.5 / lats)) * tops[j + 1]
             block = block + jnp.where(row == own - 1, edge, 0.0)
-        blocks[j] = block
+        blocks.append(block)
     coefs = jnp.concatenate(blocks, axis=0)
     every = lax.dot_general(
         green[...].reshape(degrees * layers, layers), coefs, NN, precision=lax.Precision.HIGHEST, preferred_element_type=F32
@@ -220,10 +252,15 @@
         phi = jnp.where(mine, every[n * layers : (n + 1) * layers], phi)
     above = jnp.where(row == layers - 1, 0.0, pltpu.roll(phi, layers - 1, 0))
     below = jnp.where(row == 0, 0.0, pltpu.roll(phi, 1, 0))
-    step = ((above - below) * 0.5).astype(BF16)
+    step = (above - below) * 0.5
     for j in range(rads):
+        parts = [step[n : n + QUARTER] for n in range(j * own, (j + 1) * own, QUARTER)]
+        parts[0] = jnp.where(at < chunk, parts[0], pltpu.roll(parts[3], chunk, 1))
+        parts[1] = jnp.where(at < chunk, parts[1], behind(parts[3], chunk))
+        parts = [x.astype(BF16) for x in parts[:3]]
         for i in range(lats):
-            send[i * rads + j] = step[j * own : (j + 1) * own]
+            for n, part in enumerate(parts):
+                send[i * rads + j, n] = part
 
 
 def final_kernel(recv, one, two, sizes, *, nodes):
@@ -254,7 +291,7 @@
 
     dens = dens_ref.reshape(1, own)
     field = pltpu.VMEM((own, columns), F32)
-    packet = pltpu.VMEM((devices, own, LANES), BF16)
+    packet = pltpu.VMEM((devices, 3, QUARTER, LANES), BF16)
 
     def call(name, kernel, args, out_shape, **more):
         def body(*refs):
@@ -301,13 +338,14 @@
     )
     totals = []
     for it in range(ITERS):
-        send, total = call(
+        wanted = [pltpu.VMEM((8, LANES), F32)] * (it > 0)
+        send, *total = call(
             "harmonic",
             harmonic_kernel,
             (lats, rads, chunk, degrees, lows),
-            (packet, pltpu.VMEM((8, LANES), F32)),
+            (packet, *wanted),
         )(exchange(send), mine)
-        totals.append(total)
+        totals.extend(total)
         recv = exchange(send)
         if it < ITERS - 1:
             u, send, change = call("middle", middle_kernel, (chunk,), (field, packet, field))(
@@ -330,7 +368,7 @@
         (),
         jax.ShapeDtypeStruct((ITERS,), F32),
         out_specs=pl.BlockSpec(memory_space=pltpu.SMEM),
-    )(exchange(send), totals[1], totals[2])
+    )(exchange(send), *totals)
     return (relaxed, sizes)
 
 

time: 88.8 us -> 84.4 us (0.950)
  blocking collectives: 74.1 us -> 71.2 us
  Pallas kernels: 13.6 us -> 12.2 us
    all_to_all x7, blocking collectives: 74.1 us -> 71.2 us  [exchange(): return lax.all_to_all(x, both, 0, 0, tiled=True)]
    pallas_call x1, Pallas kernels: 5.25 us -> 3.96 us  [local(): call('first', first_kernel, (chunk, lows), (field, field, field, field, p...]
where the time goes in v3:
time: 84.4 us; the launch traced here: 84.1 us
  blocking collectives  71.2 us (84%)
  Pallas kernels  12.2 us (14%)
    all_to_all x7, blocking collectives, exchange(): return lax.all_to_all(x, both, 0, 0, tiled=True)  71.2 us
    pallas_call x2, Pallas kernels, local(): call('middle', middle_kernel, (chunk,), (field, packet, field))  4.59 us
    pallas_call x1, Pallas kernels, local(): call('first', first_kernel, (chunk, lows), (field, field, field, field, p...  3.96 us
    pallas_call x3, Pallas kernels, local(): call('harmonic', harmonic_kernel, (lats, rads, chunk, degrees, lows), (pa...  1.8 us

profile of v3, /device:TPU:0, one launch (start us, length us, event | category | flops | bytes accessed | tf_op | source)
XLA Modules:
  0.0 84.1 jit_solution(15112148617490257429)
XLA Ops:
  0.6 4.0 %first.1 = (f32[16,768]{1,0:T(8,128)S(1)}, f32[16,768]{1,0:T(8,128)S(1)}, f32[16,768]{1,0:T(8,128)S(1)}, f32[16,768]{1,0:T(8,128)S(1)}, f32[1,16]{1,0:T(1,128)S(...) custom-call(f32[16,768]{1,0:T(8,128)} %refs_0_.1, ...), custom_call_target="tpu_custom_call" | custom-call | tf_op jit(solution)/shard_map/first/pallas_call | solution.py:312
  4.6 14.9 %all_to_all.35.refs_0_ = bf16[32,3,4,128]{3,2,1,0:T(4,128)(2,1)S(1)} all-to-all(bf16[32,3,4,128]{3,2,1,0:T(4,128)(2,1)S(1)} %get-tuple-element.24), channel_id=1, replica_groups=mesh['lat'=8,'rad'=4] {'lat','rad'}, dimensions={0} | all-to-all | bytes 196608 | tf_op jit(solution)/shard_map/all_to_all | solution.py:309
  19.5 0.6 harmonic.3
  20.1 9.5 %all_to_all.36.refs_0_ = bf16[32,3,4,128]{3,2,1,0:T(4,128)(2,1)S(1)} all-to-all(bf16[32,3,4,128]{3,2,1,0:T(4,128)(2,1)S(1)} %harmonic.3), channel_id=1, replica_groups=mesh['lat'=8,'rad'=4] {'lat','rad'}, dimensions={0} | all-to-all | bytes 196608 | tf_op jit(solution)/shard_map/all_to_all | solution.py:309
  29.6 2.3 %middle.2 = (f32[16,768]{1,0:T(8,128)S(1)}, bf16[32,3,4,128]{3,2,1,0:T(4,128)(2,1)S(1)}, f32[16,768]{1,0:T(8,128)S(1)}) custom-call(bf16[32,3,4,128]{3,2,1,0:T(4,128)(2,1)S(1)} %all_to_all.36.refs_0_, f32[16,768]{1,0:T(8,128)S(1)} %get-tuple-element.26.refs_1_, f32[16,768]{1,0:T(8,128)S(1)} %get-tuple-element.27.refs_2_, ...), custom_call_target="tpu_custom_call" | custom-call | tf_op jit(solution)/shard_map/middle/pallas_call | solution.py:351
  31.9 9.5 %all_to_all.37.refs_0_ = bf16[32,3,4,128]{3,2,1,0:T(4,128)(2,1)S(1)} all-to-all(bf16[32,3,4,128]{3,2,1,0:T(4,128)(2,1)S(1)} %get-tuple-element.34), channel_id=1, replica_groups=mesh['lat'=8,'rad'=4] {'lat','rad'}, dimensions={0} | all-to-all | bytes 196608 | tf_op jit(solution)/shard_map/all_to_all | solution.py:309
  41.4 0.6 harmonic.4
  42.0 9.5 %all_to_all.38.refs_0_ = bf16[32,3,4,128]{3,2,1,0:T(4,128)(2,1)S(1)} all-to-all(bf16[32,3,4,128]{3,2,1,0:T(4,128)(2,1)S(1)} %get-tuple-element.35), channel_id=1, replica_groups=mesh['lat'=8,'rad'=4] {'lat','rad'}, dimensions={0} | all-to-all | bytes 196608 | tf_op jit(solution)/shard_map/all_to_all | solution.py:309
  51.5 2.3 %middle.3 = (f32[16,768]{1,0:T(8,128)S(1)}, bf16[32,3,4,128]{3,2,1,0:T(4,128)(2,1)S(1)}, f32[16,768]{1,0:T(8,128)S(1)}) custom-call(bf16[32,3,4,128]{3,2,1,0:T(4,128)(2,1)S(1)} %all_to_all.38.refs_0_, f32[16,768]{1,0:T(8,128)S(1)} %get-tuple-element.36.refs_1_, f32[16,768]{1,0:T(8,128)S(1)} %get-tuple-element.37.refs_2_, ...), custom_call_target="tpu_custom_call" | custom-call | tf_op jit(solution)/shard_map/middle/pallas_call | solution.py:351
  53.8 9.5 %all_to_all.39.refs_0_ = bf16[32,3,4,128]{3,2,1,0:T(4,128)(2,1)S(1)} all-to-all(bf16[32,3,4,128]{3,2,1,0:T(4,128)(2,1)S(1)} %get-tuple-element.38), channel_id=1, replica_groups=mesh['lat'=8,'rad'=4] {'lat','rad'}, dimensions={0} | all-to-all | bytes 196608 | tf_op jit(solution)/shard_map/all_to_all | solution.py:309
  63.3 0.6 harmonic.5
  63.9 9.5 %all_to_all.40.refs_0_ = bf16[32,3,4,128]{3,2,1,0:T(4,128)(2,1)S(1)} all-to-all(bf16[32,3,4,128]{3,2,1,0:T(4,128)(2,1)S(1)} %get-tuple-element.39), channel_id=1, replica_groups=mesh['lat'=8,'rad'=4] {'lat','rad'}, dimensions={0} | all-to-all | bytes 196608 | tf_op jit(solution)/shard_map/all_to_all | solution.py:309
  73.3 1.3 %last.1 = (f32[16,768]{1,0:T(8,128)}, f32[32,1,128]{2,1,0:T(1,128)S(1)}) custom-call(bf16[32,3,4,128]{3,2,1,0:T(4,128)(2,1)S(1)} %all_to_all.40.refs_0_, f32[16,768]{1,0:T(8,128)S(1)} %get-tuple-element.40.refs_1_, f32[16,768]{1,0:T(8,128)S(1)} %get-tuple-element.41.refs_2_, f32[16,768]{1,0:T(8,128)S(1)} %get-tuple-element.29.refs_4_.refs_3_, ...), custom_call_target="tpu_custom_call" | custom-call | tf_op jit(solution)/shard_map/last/pallas_call | solution.py:355
  74.6 8.9 %all_to_all.41.refs_0_ = f32[32,1,128]{2,1,0:T(1,128)S(1)} all-to-all(f32[32,1,128]{2,1,0:T(1,128)S(1)} %get-tuple-element.43), channel_id=1, replica_groups=mesh['lat'=8,'rad'=4] {'lat','rad'}, dimensions={0} | all-to-all | bytes 32768 | tf_op jit(solution)/shard_map/all_to_all | solution.py:309
  83.5 0.6 final.1

commit v4 on v3

--- a/solution.py
+++ b/solution.py
@@ -37,22 +37,6 @@
         parts.append(part)
         x = x - part.astype(F32)
     return parts
-
-
-def build_counts(nb_ref, counts_ref):
-    tile = counts_ref.shape[1]
-    rows = 32
-
-    def body(b, carry):
-        at = pl.multiple_of(b * rows, rows)
-        source = lax.broadcasted_iota(jnp.int32, (rows, tile), 0) + at
-        total = jnp.zeros((rows, tile), F32)
-        for j in range(nb_ref.shape[0]):
-            total = total + (source == nb_ref[j : j + 1, :]).astype(F32)
-        counts_ref[pl.ds(at, rows), :] = total.astype(BF16)
-        return carry
-
-    lax.fori_loop(0, tile // rows, body, 0)
 
 
 def column(row_ref, rows):
@@ -148,16 +132,27 @@
     return u_ref[...] + change, total_of(change * change)
 
 
-def lateral(u, load, rate, counts):
-    rows = u.shape[0]
-    parts = jnp.concatenate(bf16_parts(u, 3), axis=0)
-    sums = lax.dot_general(parts, counts[...], NN, preferred_element_type=F32)
-    lap = sums[:rows] + sums[rows : 2 * rows] + sums[2 * rows :] - 4.0 * u
+def lateral(u, load, rate, nb_ref):
+    rows, columns = u.shape
+    blocks = [u[:, at : at + LANES] for at in range(0, columns, LANES)]
+    sums = []
+    for at in range(0, columns, LANES):
+        total = None
+        for j in range(nb_ref.shape[0]):
+            index = jnp.broadcast_to(nb_ref[j : j + 1, at : at + LANES], (rows, LANES))
+            inner, outer = lax.rem(index, LANES), lax.div(index, LANES)
+            value = jnp.take_along_axis(blocks[0], inner, axis=1)
+            for n in range(1, len(blocks)):
+                picked = jnp.take_along_axis(blocks[n], inner, axis=1)
+                value = jnp.where(outer == n, picked, value)
+            total = value if total is None else total + value
+        sums.append(total)
+    lap = jnp.concatenate(sums, axis=1) - 4.0 * u
     return rate[...] * (load[...] + lap - u)
 
 
 def first_kernel(chunk, lows, *refs):
-    sources, (counts, change, send, sems) = refs[:8], refs[16:]
+    sources, (change, send, sems) = refs[:8], refs[16:]
     targets = refs[8:16]
     u, load, grad, rate, dens, nb, mine, basis = targets
     green = sources[6]
@@ -170,30 +165,27 @@
     groups = chunks_of(slots, GROUP * chunk)
     for start, end in groups:
         copies.append((sources[7].at[start:end], basis.at[start:end]))
-    order = [5, 0, 2, 4] + list(range(7, len(copies))) + [1, 3, 6]
+    order = [0, 5, 2, 4, 1, 3] + list(range(7, len(copies))) + [6]
     copies = [pltpu.make_async_copy(*c, sems.at[n]) for n, c in enumerate(copies)]
     for n in order:
         copies[n].start()
-    copies[5].wait()
-    build_counts(nb, counts)
-    for n in (0, 2, 4):
+    for n in (0, 2, 4, 5, 1, 3):
         copies[n].wait()
+    change[...] = lateral(u[...], load, rate, nb)
 
     def ready(d):
         if d % GROUP == 0:
             copies[7 + d // GROUP].wait()
 
     analyse(u[...], grad, dens, basis, send, None, chunk, ready)
-    for n in (1, 3, 6):
-        copies[n].wait()
-    change[...] = lateral(u[...], load, rate, counts)
-
-
-def middle_kernel(chunk, recv, change, u, load, rate, grad, dens, basis, counts, u_out, send, later):
+    copies[6].wait()
+
+
+def middle_kernel(chunk, recv, change, u, load, rate, grad, dens, basis, nb, u_out, send, later):
     new, squares = advance(recv, change, u, rate, basis, chunk)
     u_out[...] = new
     analyse(new, grad, dens, basis, send, squares, chunk)
-    later[...] = lateral(new, load, rate, counts)
+    later[...] = lateral(new, load, rate, nb)
 
 
 def last_kernel(chunk, recv, change, u, rate, basis, relaxed, send):
@@ -309,7 +301,7 @@
         return lax.all_to_all(x, both, 0, 0, tiled=True)
 
     groups = len(chunks_of(slots, GROUP * chunk))
-    u, load, grad, rate, dens, _, mine, basis, counts, change, send = call(
+    u, load, grad, rate, dens, nb, mine, basis, change, send = call(
         "first",
         first_kernel,
         (chunk, lows),
@@ -322,7 +314,6 @@
             pltpu.VMEM(neighbours.shape, jnp.int32),
             pltpu.VMEM((degrees, L, L), F32),
             pltpu.VMEM(basis.shape, BF16),
-            pltpu.VMEM((columns, columns), BF16),
             field,
             packet,
         ),
@@ -349,7 +340,7 @@
         recv = exchange(send)
         if it < ITERS - 1:
             u, send, change = call("middle", middle_kernel, (chunk,), (field, packet, field))(
-                recv, change, u, load, rate, grad, dens, basis, counts
+                recv, change, u, load, rate, grad, dens, basis, nb
             )
         else:
             relaxed, send = call(

time: 84.4 us -> 83.3 us (0.987)
  Pallas kernels: 12.2 us -> 11.2 us
where the time goes in v4:
time: 83.3 us; the launch traced here: 83.1 us
  blocking collectives  71.2 us (85%)
  Pallas kernels  11.2 us (13%)
    all_to_all x7, blocking collectives, exchange(): return lax.all_to_all(x, both, 0, 0, tiled=True)  71.2 us
    pallas_call x2, Pallas kernels, local(): call('middle', middle_kernel, (chunk,), (field, packet, field))  4.32 us
    pallas_call x1, Pallas kernels, local(): call('first', first_kernel, (chunk, lows), (field, field, field, field, p...  3.19 us
    pallas_call x3, Pallas kernels, local(): call('harmonic', harmonic_kernel, (lats, rads, chunk, degrees, lows), (pa...  1.81 us

profile of v4, /device:TPU:0, one launch (start us, length us, event | category | flops | bytes accessed | tf_op | source)
XLA Modules:
  0.0 83.1 jit_solution(15401163314000665696)
XLA Ops:
  0.6 3.2 %first.1 = (f32[16,768]{1,0:T(8,128)S(1)}, f32[16,768]{1,0:T(8,128)S(1)}, f32[16,768]{1,0:T(8,128)S(1)}, f32[16,768]{1,0:T(8,128)S(1)}, f32[1,16]{1,0:T(1,128)S(...) custom-call(f32[16,768]{1,0:T(8,128)} %refs_0_.1, ...), custom_call_target="tpu_custom_call" | custom-call | tf_op jit(solution)/shard_map/first/pallas_call | solution.py:304
  3.8 14.9 %all_to_all.35.refs_0_ = bf16[32,3,4,128]{3,2,1,0:T(4,128)(2,1)S(1)} all-to-all(bf16[32,3,4,128]{3,2,1,0:T(4,128)(2,1)S(1)} %get-tuple-element.24), channel_id=1, replica_groups=mesh['lat'=8,'rad'=4] {'lat','rad'}, dimensions={0} | all-to-all | bytes 196608 | tf_op jit(solution)/shard_map/all_to_all | solution.py:301
  18.8 0.6 harmonic.3
  19.4 9.5 %all_to_all.36.refs_0_ = bf16[32,3,4,128]{3,2,1,0:T(4,128)(2,1)S(1)} all-to-all(bf16[32,3,4,128]{3,2,1,0:T(4,128)(2,1)S(1)} %harmonic.3), channel_id=1, replica_groups=mesh['lat'=8,'rad'=4] {'lat','rad'}, dimensions={0} | all-to-all | bytes 196608 | tf_op jit(solution)/shard_map/all_to_all | solution.py:301
  28.9 2.2 %middle.2 = (f32[16,768]{1,0:T(8,128)S(1)}, bf16[32,3,4,128]{3,2,1,0:T(4,128)(2,1)S(1)}, f32[16,768]{1,0:T(8,128)S(1)}) custom-call(bf16[32,3,4,128]{3,2,1,0:T(4,128)(2,1)S(1)} %all_to_all.36.refs_0_, f32[16,768]{1,0:T(8,128)S(1)} %get-tuple-element.26.refs_1_, f32[16,768]{1,0:T(8,128)S(1)} %get-tuple-element.27.refs_2_, ...), custom_call_target="tpu_custom_call" | custom-call | tf_op jit(solution)/shard_map/middle/pallas_call | solution.py:342
  31.0 9.5 %all_to_all.37.refs_0_ = bf16[32,3,4,128]{3,2,1,0:T(4,128)(2,1)S(1)} all-to-all(bf16[32,3,4,128]{3,2,1,0:T(4,128)(2,1)S(1)} %get-tuple-element.34), channel_id=1, replica_groups=mesh['lat'=8,'rad'=4] {'lat','rad'}, dimensions={0} | all-to-all | bytes 196608 | tf_op jit(solution)/shard_map/all_to_all | solution.py:301
  40.5 0.6 harmonic.4
  41.1 9.5 %all_to_all.38.refs_0_ = bf16[32,3,4,128]{3,2,1,0:T(4,128)(2,1)S(1)} all-to-all(bf16[32,3,4,128]{3,2,1,0:T(4,128)(2,1)S(1)} %get-tuple-element.35), channel_id=1, replica_groups=mesh['lat'=8,'rad'=4] {'lat','rad'}, dimensions={0} | all-to-all | bytes 196608 | tf_op jit(solution)/shard_map/all_to_all | solution.py:301
  50.6 2.2 %middle.3 = (f32[16,768]{1,0:T(8,128)S(1)}, bf16[32,3,4,128]{3,2,1,0:T(4,128)(2,1)S(1)}, f32[16,768]{1,0:T(8,128)S(1)}) custom-call(bf16[32,3,4,128]{3,2,1,0:T(4,128)(2,1)S(1)} %all_to_all.38.refs_0_, f32[16,768]{1,0:T(8,128)S(1)} %get-tuple-element.36.refs_1_, f32[16,768]{1,0:T(8,128)S(1)} %get-tuple-element.37.refs_2_, ...), custom_call_target="tpu_custom_call" | custom-call | tf_op jit(solution)/shard_map/middle/pallas_call | solution.py:342
  52.7 9.5 %all_to_all.39.refs_0_ = bf16[32,3,4,128]{3,2,1,0:T(4,128)(2,1)S(1)} all-to-all(bf16[32,3,4,128]{3,2,1,0:T(4,128)(2,1)S(1)} %get-tuple-element.38), channel_id=1, replica_groups=mesh['lat'=8,'rad'=4] {'lat','rad'}, dimensions={0} | all-to-all | bytes 196608 | tf_op jit(solution)/shard_map/all_to_all | solution.py:301
  62.2 0.6 harmonic.5
  62.8 9.5 %all_to_all.40.refs_0_ = bf16[32,3,4,128]{3,2,1,0:T(4,128)(2,1)S(1)} all-to-all(bf16[32,3,4,128]{3,2,1,0:T(4,128)(2,1)S(1)} %get-tuple-element.39), channel_id=1, replica_groups=mesh['lat'=8,'rad'=4] {'lat','rad'}, dimensions={0} | all-to-all | bytes 196608 | tf_op jit(solution)/shard_map/all_to_all | solution.py:301
  72.3 1.3 %last.1 = (f32[16,768]{1,0:T(8,128)}, f32[32,1,128]{2,1,0:T(1,128)S(1)}) custom-call(bf16[32,3,4,128]{3,2,1,0:T(4,128)(2,1)S(1)} %all_to_all.40.refs_0_, f32[16,768]{1,0:T(8,128)S(1)} %get-tuple-element.40.refs_1_, f32[16,768]{1,0:T(8,128)S(1)} %get-tuple-element.41.refs_2_, f32[16,768]{1,0:T(8,128)S(1)} %get-tuple-element.29.refs_4_.refs_3_, ...), custom_call_target="tpu_custom_call" | custom-call | tf_op jit(solution)/shard_map/last/pallas_call | solution.py:346
  73.6 8.9 %all_to_all.41.refs_0_ = f32[32,1,128]{2,1,0:T(1,128)S(1)} all-to-all(f32[32,1,128]{2,1,0:T(1,128)S(1)} %get-tuple-element.43), channel_id=1, replica_groups=mesh['lat'=8,'rad'=4] {'lat','rad'}, dimensions={0} | all-to-all | bytes 32768 | tf_op jit(solution)/shard_map/all_to_all | solution.py:301
  82.5 0.6 final.1

commit v5 on v4

--- a/solution.py
+++ b/solution.py
@@ -152,7 +152,7 @@
 
 
 def first_kernel(chunk, lows, *refs):
-    sources, (change, send, sems) = refs[:8], refs[16:]
+    sources, (parts, change, send, sems) = refs[:8], refs[16:]
     targets = refs[8:16]
     u, load, grad, rate, dens, nb, mine, basis = targets
     green = sources[6]
@@ -162,23 +162,28 @@
     for source, target in zip(sources[:6], targets[:6]):
         copies.append((source, target))
     copies.append((green.at[pl.ds(lows(device), mine.shape[0])], mine))
-    groups = chunks_of(slots, GROUP * chunk)
+    pieces, groups = chunks_of(slots, chunk), chunks_of(slots, GROUP * chunk)
     for start, end in groups:
         copies.append((sources[7].at[start:end], basis.at[start:end]))
-    order = [0, 5, 2, 4, 1, 3] + list(range(7, len(copies))) + [6]
+    order = [0, 2, 4, 7, 5, 1, 3, 6] + list(range(8, len(copies)))
     copies = [pltpu.make_async_copy(*c, sems.at[n]) for n, c in enumerate(copies)]
     for n in order:
         copies[n].start()
-    for n in (0, 2, 4, 5, 1, 3):
+    for n in (0, 2, 4):
         copies[n].wait()
-    change[...] = lateral(u[...], load, rate, nb)
 
     def ready(d):
         if d % GROUP == 0:
             copies[7 + d // GROUP].wait()
+        if d + GROUP >= len(pieces) and d % GROUP == 0:
+            for n in (5, 1, 3, 6):
+                copies[n].wait()
+            change[...] = lateral(u[...], load, rate, nb)
+            flat = mine[...].reshape(parts.shape[0], mine.shape[2])
+            high, low = [x.astype(F32) for x in bf16_parts(flat, 2)]
+            parts[...] = jnp.concatenate([high, low], axis=1).astype(BF16)
 
     analyse(u[...], grad, dens, basis, send, None, chunk, ready)
-    copies[6].wait()
 
 
 def middle_kernel(chunk, recv, change, u, load, rate, grad, dens, basis, nb, u_out, send, later):
@@ -230,8 +235,10 @@
             block = block + jnp.where(row == own - 1, edge, 0.0)
         blocks.append(block)
     coefs = jnp.concatenate(blocks, axis=0)
+    high, low = bf16_parts(coefs, 2)
+    halves = [jnp.concatenate([high, x], axis=1) for x in (low, jnp.zeros_like(low))]
     every = lax.dot_general(
-        green[...].reshape(degrees * layers, layers), coefs, NN, precision=lax.Precision.HIGHEST, preferred_element_type=F32
+        green[...], jnp.concatenate(halves, axis=0), NN, preferred_element_type=F32
     )
     lane = lax.broadcasted_iota(jnp.int32, (layers, LANES), 1)
     row = lax.broadcasted_iota(jnp.int32, (layers, LANES), 0)
@@ -241,7 +248,8 @@
     for n in range(degrees):
         degree = start + n
         mine = (k >= degree * degree) & (k < (degree + 1) * (degree + 1)) & (lane < chunk)
-        phi = jnp.where(mine, every[n * layers : (n + 1) * layers], phi)
+        rows = every[n * layers : (n + 1) * layers]
+        phi = jnp.where(mine, rows[:, :LANES] + rows[:, LANES:], phi)
     above = jnp.where(row == layers - 1, 0.0, pltpu.roll(phi, layers - 1, 0))
     below = jnp.where(row == 0, 0.0, pltpu.roll(phi, 1, 0))
     step = (above - below) * 0.5
@@ -301,7 +309,7 @@
         return lax.all_to_all(x, both, 0, 0, tiled=True)
 
     groups = len(chunks_of(slots, GROUP * chunk))
-    u, load, grad, rate, dens, nb, mine, basis, change, send = call(
+    u, load, grad, rate, dens, nb, _, basis, mine, change, send = call(
         "first",
         first_kernel,
         (chunk, lows),
@@ -314,6 +322,7 @@
             pltpu.VMEM(neighbours.shape, jnp.int32),
             pltpu.VMEM((degrees, L, L), F32),
             pltpu.VMEM(basis.shape, BF16),
+            pltpu.VMEM((degrees * L, 2 * L), BF16),
             field,
             packet,
         ),

time: 83.3 us -> 82.9 us (level)
  no operation moved by 1% of the time
where the time goes in v5:
time: 82.9 us; the launch traced here: 82.7 us
  blocking collectives  71.2 us (86%)
  Pallas kernels  10.9 us (13%)
    all_to_all x7, blocking collectives, exchange(): return lax.all_to_all(x, both, 0, 0, tiled=True)  71.2 us
    pallas_call x2, Pallas kernels, local(): call('middle', middle_kernel, (chunk,), (field, packet, field))  4.31 us
    pallas_call x1, Pallas kernels, local(): call('first', first_kernel, (chunk, lows), (field, field, field, field, p...  3.29 us

profile of v5, /device:TPU:0, one launch (start us, length us, event | category | flops | bytes accessed | tf_op | source)
XLA Modules:
  0.0 82.7 jit_solution(14054421127082481711)
XLA Ops:
  0.6 3.3 %first.1 = (f32[16,768]{1,0:T(8,128)S(1)}, f32[16,768]{1,0:T(8,128)S(1)}, f32[16,768]{1,0:T(8,128)S(1)}, f32[16,768]{1,0:T(8,128)S(1)}, f32[1,16]{1,0:T(1,128)S(...) custom-call(f32[16,768]{1,0:T(8,128)} %refs_0_.1, ...), custom_call_target="tpu_custom_call" | custom-call | tf_op jit(solution)/shard_map/first/pallas_call | solution.py:312
  3.9 14.9 %all_to_all.35.refs_0_ = bf16[32,3,4,128]{3,2,1,0:T(4,128)(2,1)S(1)} all-to-all(bf16[32,3,4,128]{3,2,1,0:T(4,128)(2,1)S(1)} %get-tuple-element.24), channel_id=1, replica_groups=mesh['lat'=8,'rad'=4] {'lat','rad'}, dimensions={0} | all-to-all | bytes 196608 | tf_op jit(solution)/shard_map/all_to_all | solution.py:309
  18.8 0.5 harmonic.3
  19.3 9.5 %all_to_all.36.refs_0_ = bf16[32,3,4,128]{3,2,1,0:T(4,128)(2,1)S(1)} all-to-all(bf16[32,3,4,128]{3,2,1,0:T(4,128)(2,1)S(1)} %harmonic.3), channel_id=1, replica_groups=mesh['lat'=8,'rad'=4] {'lat','rad'}, dimensions={0} | all-to-all | bytes 196608 | tf_op jit(solution)/shard_map/all_to_all | solution.py:309
  28.8 2.2 %middle.2 = (f32[16,768]{1,0:T(8,128)S(1)}, bf16[32,3,4,128]{3,2,1,0:T(4,128)(2,1)S(1)}, f32[16,768]{1,0:T(8,128)S(1)}) custom-call(bf16[32,3,4,128]{3,2,1,0:T(4,128)(2,1)S(1)} %all_to_all.36.refs_0_, f32[16,768]{1,0:T(8,128)S(1)} %get-tuple-element.26.refs_1_, f32[16,768]{1,0:T(8,128)S(1)} %get-tuple-element.27.refs_2_, ...), custom_call_target="tpu_custom_call" | custom-call | tf_op jit(solution)/shard_map/middle/pallas_call | solution.py:351
  30.9 9.5 %all_to_all.37.refs_0_ = bf16[32,3,4,128]{3,2,1,0:T(4,128)(2,1)S(1)} all-to-all(bf16[32,3,4,128]{3,2,1,0:T(4,128)(2,1)S(1)} %get-tuple-element.34), channel_id=1, replica_groups=mesh['lat'=8,'rad'=4] {'lat','rad'}, dimensions={0} | all-to-all | bytes 196608 | tf_op jit(solution)/shard_map/all_to_all | solution.py:309
  40.4 0.4 harmonic.4
  40.9 9.5 %all_to_all.38.refs_0_ = bf16[32,3,4,128]{3,2,1,0:T(4,128)(2,1)S(1)} all-to-all(bf16[32,3,4,128]{3,2,1,0:T(4,128)(2,1)S(1)} %get-tuple-element.35), channel_id=1, replica_groups=mesh['lat'=8,'rad'=4] {'lat','rad'}, dimensions={0} | all-to-all | bytes 196608 | tf_op jit(solution)/shard_map/all_to_all | solution.py:309
  50.4 2.2 %middle.3 = (f32[16,768]{1,0:T(8,128)S(1)}, bf16[32,3,4,128]{3,2,1,0:T(4,128)(2,1)S(1)}, f32[16,768]{1,0:T(8,128)S(1)}) custom-call(bf16[32,3,4,128]{3,2,1,0:T(4,128)(2,1)S(1)} %all_to_all.38.refs_0_, f32[16,768]{1,0:T(8,128)S(1)} %get-tuple-element.36.refs_1_, f32[16,768]{1,0:T(8,128)S(1)} %get-tuple-element.37.refs_2_, ...), custom_call_target="tpu_custom_call" | custom-call | tf_op jit(solution)/shard_map/middle/pallas_call | solution.py:351
  52.5 9.5 %all_to_all.39.refs_0_ = bf16[32,3,4,128]{3,2,1,0:T(4,128)(2,1)S(1)} all-to-all(bf16[32,3,4,128]{3,2,1,0:T(4,128)(2,1)S(1)} %get-tuple-element.38), channel_id=1, replica_groups=mesh['lat'=8,'rad'=4] {'lat','rad'}, dimensions={0} | all-to-all | bytes 196608 | tf_op jit(solution)/shard_map/all_to_all | solution.py:309
  62.0 0.5 harmonic.5
  62.4 9.5 %all_to_all.40.refs_0_ = bf16[32,3,4,128]{3,2,1,0:T(4,128)(2,1)S(1)} all-to-all(bf16[32,3,4,128]{3,2,1,0:T(4,128)(2,1)S(1)} %get-tuple-element.39), channel_id=1, replica_groups=mesh['lat'=8,'rad'=4] {'lat','rad'}, dimensions={0} | all-to-all | bytes 196608 | tf_op jit(solution)/shard_map/all_to_all | solution.py:309
  71.9 1.3 %last.1 = (f32[16,768]{1,0:T(8,128)}, f32[32,1,128]{2,1,0:T(1,128)S(1)}) custom-call(bf16[32,3,4,128]{3,2,1,0:T(4,128)(2,1)S(1)} %all_to_all.40.refs_0_, f32[16,768]{1,0:T(8,128)S(1)} %get-tuple-element.40.refs_1_, f32[16,768]{1,0:T(8,128)S(1)} %get-tuple-element.41.refs_2_, f32[16,768]{1,0:T(8,128)S(1)} %get-tuple-element.29.refs_4_.refs_3_, ...), custom_call_target="tpu_custom_call" | custom-call | tf_op jit(solution)/shard_map/last/pallas_call | solution.py:355
  73.2 8.9 %all_to_all.41.refs_0_ = f32[32,1,128]{2,1,0:T(1,128)S(1)} all-to-all(f32[32,1,128]{2,1,0:T(1,128)S(1)} %get-tuple-element.43), channel_id=1, replica_groups=mesh['lat'=8,'rad'=4] {'lat','rad'}, dimensions={0} | all-to-all | bytes 32768 | tf_op jit(solution)/shard_map/all_to_all | solution.py:309
  82.1 0.6 final.1
